TPU v7x, 32 devices: a whole 2x2x4 slice. The times are simulated.
32 devices in a mesh: section: 2 (over core), dp: 4 (over z), tensor: 4 (over y, x).
Axes of the slice: x: 2, y: 2, z: 4, core: 2. Of those that a mesh axis runs over, the one named last changes fastest.
Arguments:
- inputs: bfloat16 [2, 512, 4096], P(None, 'dp', 'tensor'), may hold values from -6 to 6
- adapter_down: bfloat16 [2, 4096, 128], P('section', 'tensor'), may hold values from -0.09375 to 0.09375
- adapter_up: bfloat16 [2, 128, 4096], P('section', None, 'tensor'), may hold values from -0.5 to 0.5
- gains: bfloat16 [2, 4096], P('section', 'tensor'), may hold values from 0.25 to 1.75
- head: bfloat16 [4096, 128], P('tensor'), may hold values from -0.375 to 0.375
- labels: int32 [2, 512], P(None, 'dp'), may hold values from 0 to 127
- valid: int32 [2, 512], P(None, 'dp'), may hold values from 0 to 1, as said below
Outputs:
- grads_down: float32 [2, 4096, 128], P('section', 'tensor', 'dp')
- grads_up: float32 [2, 128, 4096], P('section', 'dp', 'tensor')
- grads_gain: float32 [2, 4096], P('section', 'tensor')
Inputs may be any that keep to these rules, and one draw needn't show every extreme that they name: In each microbatch the first of every 128 consecutive tokens is valid.
All inputs are finite; a program needn't handle non-finite values.
Results may differ from a plain program's by a relative error of at most 0.015.
Values may be sent and summed in bfloat16 or wider, within the bound.
A program may use at most 64 MiB of HBM per device.

v0:
```python
import functools

import jax
import jax.numpy as jnp
from jax import lax
from jax.experimental import pallas as pl
from jax.experimental.pallas import tpu as pltpu
from jax.sharding import PartitionSpec as P

MESH = pl.DeviceIdType.MESH
epsilon = 1e-05
F32 = jnp.float32
BF16 = jnp.bfloat16


def mm(a, b):
    return jnp.dot(a, b, preferred_element_type=F32)


def mm_nt(a, b):
    return lax.dot_general(a, b, (((1,), (1,)), ((), ())), preferred_element_type=F32)


def mm_tn(a, b):
    return lax.dot_general(a, b, (((0,), (0,)), ((), ())), preferred_element_type=F32)


def split(v):
    high = v.astype(BF16)
    return high, (v - high.astype(F32)).astype(BF16)


def kernel(
    nt, nd, width,
    x_hbm, dn_hbm, up_hbm, gain_hbm, head_hbm, lab_hbm, val_hbm,
    out,
    x_ref, dn_ref, up_ref, gain_ref, head_ref, lab_ref, val_ref,
    odn, oup, ogain, stok, rtok, sgram, rgram, pgram, gall, sres, res, sdp, rdp, rin, relay, psum, rcross, sgn, rgn,
    load, sib_s, sib_r, tok_s, tok_r, gr_s, gr_r, ga_s, ga_r, re_s, re_r, fw_s, fw_r, dp_s, dp_r, rel_s, rel_r, cr_s, cr_r,
):
    s, d, t = lax.axis_index("section"), lax.axis_index("dp"), lax.axis_index("tensor")
    first = s == 0
    tokens, feats = x_ref.shape
    rank = dn_ref.shape[1]
    half = tokens // 2
    own = half // nt
    rows = rank // nt
    part = rank // nd
    wire = stok.dtype

    def peer(k, other):
        return (1 - s if other else s, d, lax.rem(t + k, nt))

    group = [(k, o) for k in range(nt) for o in (0, 1) if (k, o) != (0, 0)]

    loads = [
        pltpu.make_async_copy(a, b, load.at[i])
        for i, (a, b) in enumerate((
            (up_hbm, up_ref), (head_hbm, head_ref), (x_hbm, x_ref), (gain_hbm, gain_ref),
            (dn_hbm, dn_ref), (lab_hbm, lab_ref), (val_hbm, val_ref),
        ))
    ]
    for c in loads:
        c.start()

    barrier = pltpu.get_barrier_semaphore()
    for k, o in group:
        pl.semaphore_signal(barrier, inc=1, device_id=peer(k, o), device_id_type=MESH)
    for k in range(1, nd):
        pl.semaphore_signal(barrier, inc=1, device_id=(s, lax.rem(d + k, nd), t), device_id_type=MESH)

    def send(src, dst, ss, rs, to):
        copy = pltpu.make_async_remote_copy(
            src_ref=src, dst_ref=dst, send_sem=ss, recv_sem=rs, device_id=to, device_id_type=MESH
        )
        copy.start()
        return copy

    def put_gram(j, g):
        g = g.astype(wire)
        for i in range(nt):
            sgram[i, j] = g[i * rows : (i + 1) * rows]

    loads[0].wait()
    up = up_ref[...]
    put_gram(0, mm_nt(up, up))
    loads[1].wait()
    head = head_ref[...]
    put_gram(1, mm(up, head))
    for c in loads[2:]:
        c.wait()
    gain = gain_ref[...].astype(F32)
    xb = x_ref[...]
    xf = xb.astype(F32)
    xup = mm_nt(xb, up).astype(wire)
    proj = mm((xf * gain).astype(BF16), dn_ref[...]).astype(wire)
    for b in range(2):
        for i in range(nt):
            at = b * half + i * own
            stok[b, i, 0] = proj[at : at + own]
            stok[b, i, 1] = xup[at : at + own]

    pl.semaphore_wait(barrier, len(group) + nd - 1)

    sib = [
        send(a, b, sib_s.at[i], sib_r.at[i], peer(0, 1))
        for i, (a, b) in enumerate(((up_ref, oup), (dn_ref, odn), (gain_ref, ogain)))
    ]
    started = list(sib)
    spans = (pl.ds(0, 2), pl.ds(2, 1))

    def scatter_gram(j):
        copies = [
            send(
                sgram.at[lax.rem(t + k, nt), spans[j]], rgram.at[k, spans[j]],
                gr_s.at[j, k], gr_r.at[j, k], peer(k, 0),
            )
            for k in range(1, nt)
        ]
        started.extend(copies)
        return copies

    def gather_gram(j, copies):
        total = sgram[t, spans[j]].astype(F32)
        for k in range(1, nt):
            copies[k - 1].wait_recv()
            total = total + rgram[k, spans[j]].astype(F32)
        total = total.astype(wire)
        pgram[spans[j]] = total
        gall[s, t, spans[j]] = total
        out_copies = [
            send(
                pgram.at[spans[j]], gall.at[s, t, spans[j]],
                ga_s.at[j, o, k], ga_r.at[j, o, k], peer(k, o),
            )
            for k, o in group
        ]
        started.extend(out_copies)
        return out_copies

    ab_copies = scatter_gram(0)
    tok_copies = {}
    for k in range(nt):
        to = lax.rem(t + k, nt)
        tok_copies[k, 1] = send(
            stok.at[1 - s, to, pl.ds(0, 2)], rtok.at[1, k, pl.ds(0, 2)],
            tok_s.at[1, k], tok_r.at[1, k], peer(k, 1),
        )
    xm = x_ref[pl.ds(pl.multiple_of(s * half, half), half), :]
    xmf = xm.astype(F32)
    xhead = mm(xm, head)
    squares = jnp.broadcast_to(jnp.sum(xmf * xmf, axis=1, keepdims=True), (half, rank))
    hh, hl = split(xhead)
    qh, ql = split(squares)
    lane_h = lax.broadcasted_iota(jnp.int32, (half, rank), 1)
    q = jnp.where(lane_h < rank // 2, qh.astype(F32), ql.astype(F32)).astype(wire)
    hh, hl = hh.astype(wire), hl.astype(wire)
    for i in range(nt):
        stok[s, i, 2] = hh[i * own : (i + 1) * own]
        stok[s, i, 3] = hl[i * own : (i + 1) * own]
        stok[s, i, 4] = q[i * own : (i + 1) * own]

    sib[0].wait_recv()
    gram_c = mm_nt(up, oup[...])
    gram_d = mm((oup[...].astype(F32) * gain).astype(BF16), dn_ref[...])
    put_gram(2, jnp.where(first, gram_c, gram_d))
    c_copies = scatter_gram(1)
    for k in range(1, nt):
        to = lax.rem(t + k, nt)
        tok_copies[k, 0] = send(
            stok.at[s, to], rtok.at[0, k], tok_s.at[0, k], tok_r.at[0, k], peer(k, 0)
        )
    started += list(tok_copies.values())
    all_copies = gather_gram(0, ab_copies)
    all_copies = all_copies + gather_gram(1, c_copies)

    lab = jnp.where(first, lab_ref[0:1, :], lab_ref[1:2, :])
    val = jnp.where(first, val_ref[0:1, :], val_ref[1:2, :]).astype(F32)
    labels_n = head.shape[1]
    hot_t = jnp.where(lax.broadcasted_iota(jnp.int32, (labels_n, half), 0) == lab, val, 0.0).astype(BF16)
    val_t = jnp.broadcast_to(val, (labels_n, half)).astype(BF16)
    pick = (
        lax.broadcasted_iota(jnp.int32, (own, half), 0) + t * own
        == lax.broadcasted_iota(jnp.int32, (own, half), 1)
    ).astype(F32).astype(BF16)
    onehot = mm_nt(pick, hot_t)
    validity = mm_nt(pick, val_t)
    count = jnp.sum(val_ref[...].astype(F32))

    mine = stok[s, t].astype(F32)
    for k in range(1, nt):
        tok_copies[k, 0].wait_recv()
        mine = mine + rtok[0, k].astype(F32)
    tok_copies[0, 1].wait_recv()
    theirs = rtok[1, 0, 0:2].astype(F32)
    for k in range(1, nt):
        tok_copies[k, 1].wait_recv()
        theirs = theirs + rtok[1, k, 0:2].astype(F32)
    p0 = jnp.where(first, mine[0], theirs[0])
    p1 = jnp.where(first, theirs[0], mine[0])
    v0 = jnp.where(first, mine[1], theirs[1])
    v1 = jnp.where(first, theirs[1], mine[1])
    xh = mine[2] + mine[3]
    sq0 = mine[4][:, 0:1] + mine[4][:, rank // 2 : rank // 2 + 1]

    for c in all_copies:
        c.wait_recv()

    def gram(a, j):
        return gall[a, :, j].reshape(rank, rank).astype(BF16)

    a0, b0, c0 = gram(0, 0), gram(0, 1), gram(0, 2)
    a1, b1, d1 = gram(1, 0), gram(1, 1), gram(1, 2)

    def rowsum(v):
        return jnp.sum(v, axis=1, keepdims=True)

    inv0 = lax.rsqrt(sq0 / width + epsilon)
    pre0 = inv0 * p0
    sig0 = jax.nn.sigmoid(pre0)
    h0 = (pre0 * sig0).astype(BF16)
    h0f = h0.astype(F32)
    h0a = mm(h0, a0)
    p1 = p1 + mm(h0, d1)
    s1u0 = v0 + h0a
    s1u1 = v1 + mm(h0, c0)
    base = xh + mm(h0, b0)
    sq1 = sq0 + rowsum(h0f * (v0 + s1u0))
    inv1 = lax.rsqrt(sq1 / width + epsilon)
    pre1 = inv1 * p1
    sig1 = jax.nn.sigmoid(pre1)
    h1 = (pre1 * sig1).astype(BF16)
    h1f = h1.astype(F32)
    yu1 = s1u1 + mm(h1, a1)
    yu0 = s1u0 + mm_nt(h1, c0)
    base = base + mm(h1, b1)
    sq2 = sq1 + rowsum(h1f * (s1u1 + yu1))
    inv2 = lax.rsqrt(sq2 / width + epsilon)
    logits = inv2 * base
    expo = jnp.exp(logits - jnp.max(logits, axis=1, keepdims=True))
    cot = expo / rowsum(expo) * validity - onehot
    radial = rowsum(cot * base)
    wh = (inv2 * cot).astype(BF16)
    ch = inv2 * inv2 * inv2 / width * radial
    hg1 = mm_nt(wh, b1) - ch * yu1
    act1 = hg1 * sig1 * (1.0 + pre1 * (1.0 - sig1))
    w1 = (inv1 * act1).astype(BF16)
    c1 = inv1 * inv1 * inv1 / width * rowsum(act1 * p1)
    hg0 = mm_nt(wh, b0) - ch * yu0 + mm_nt(w1, d1) - c1 * s1u0
    act0 = hg0 * sig0 * (1.0 + pre0 * (1.0 - sig0))
    w0 = (inv0 * act0).astype(BF16)

    ch_h, ch_l = split(ch)
    c1_h, c1_l = split(c1)
    lane = lax.broadcasted_iota(jnp.int32, (own, rank), 1)
    q4 = rank // 4
    coef = jnp.where(
        lane < q4, ch_h.astype(F32),
        jnp.where(lane < 2 * q4, ch_l.astype(F32), jnp.where(lane < 3 * q4, c1_h.astype(F32), c1_l.astype(F32))),
    )
    for j, v in enumerate((h0, h1, w0, w1, wh, coef)):
        v = v.astype(wire)
        sres[j] = v
        res[s, t, j] = v
    res_copies = {
        k: send(sres, res.at[s, t], re_s.at[k], re_r.at[k], peer(k, 0 if k else 1)) for k in range(nt)
    }
    forwards = []
    for k in range(1, nt):
        res_copies[k].wait_recv()
        at = lax.rem(t + nt - k, nt)
        forwards.append(send(res.at[s, at], res.at[s, at], fw_s.at[k], fw_r.at[k], peer(0, 1)))
    started += list(res_copies.values()) + forwards
    sib[1].wait_recv()
    sib[2].wait_recv()
    res_copies[0].wait_recv()
    for c in forwards:
        c.wait_recv()

    def got(j):
        return res[:, :, j].reshape(tokens, res.shape[-1])

    def piece(j, full):
        full = full.astype(BF16)
        for i in range(nd):
            sdp[i, j] = full[i * part : (i + 1) * part]

    hl = nd // 2
    side = d // hl
    local_d = lax.rem(d, hl)
    far = (1 - side) * hl
    odd = lax.rem(d, 2)
    outer = odd == side

    def remote(src, dst, ss, rs, to):
        return pltpu.make_async_remote_copy(
            src_ref=src, dst_ref=dst, send_sem=ss, recv_sem=rs, device_id=(s, to, t), device_id_type=MESH
        )

    def up_copy(k):
        to = lax.rem(d + k, nd)
        return remote(sdp.at[to, 1], rdp.at[k], dp_s.at[0, k], dp_r.at[0, k], to)

    def near_copy(k):
        to = side * hl + lax.rem(local_d + k, hl)
        return remote(sdp.at[to, 0], rin.at[k], dp_s.at[1, k], dp_r.at[1, k], to)

    def relay_copy():
        return remote(sdp.at[pl.ds(far, hl), 0], relay, rel_s, rel_r, d + 1 - 2 * odd)

    def cross_copy(i):
        m = local_d // 2
        return remote(psum.at[i], rcross.at[m], cr_s.at[i], cr_r.at[m], far + i)

    def cross_wait(m):
        return remote(psum.at[0], rcross.at[m], cr_s.at[0], cr_r.at[m], far)

    def finish(state, own_w, own_h, cotangent):
        scaled = (state * gain).astype(BF16)
        piece(0, mm_tn(own_w, scaled))

        @pl.when(outer)
        def _():
            relay_copy().start()

        gain_row = jnp.sum(mm_nt(own_w, dn_ref[...]) * state, axis=0, keepdims=True)
        sgn[0:1, :] = gain_row
        sgn[1:2, :] = jnp.full((1, feats), count, F32)
        piece(1, mm_tn(own_h, cotangent().astype(BF16)))
        for k in sorted(range(1, nd), key=lambda k: abs(k - hl)):
            up_copy(k).start()
        for k in range(1, hl):
            near_copy(k).start()

    h0g, h1g, w1g, whg = (got(j).astype(BF16) for j in (0, 1, 3, 4))
    cg = got(5).astype(F32)
    chg = cg[:, 0:1] + cg[:, q4 : q4 + 1]
    c1g = cg[:, 2 * q4 : 2 * q4 + 1] + cg[:, 3 * q4 : 3 * q4 + 1]

    @pl.when(s == 0)
    def _():
        def cotangent():
            s1 = xf + mm(h0g, up)
            y = s1 + mm(h1g, oup[...])
            g2 = mm_nt(whg, head) - chg * y
            return g2 + ogain[...].astype(F32) * mm_nt(w1g, odn[...]) - c1g * s1

        finish(xf, got(2).astype(BF16), h0g, cotangent)

    @pl.when(s != 0)
    def _():
        s1 = xf + mm(h0g, oup[...])

        def cotangent():
            y = s1 + mm(h1g, up)
            return mm_nt(whg, head) - chg * y

        finish(s1, w1g, h1g, cotangent)

    small_copies = [
        send(sgn, rgn.at[k], dp_s.at[2, k], dp_r.at[2, k], (s, lax.rem(d + k, nd), t)) for k in range(1, nd)
    ]
    started += small_copies

    @pl.when(jnp.logical_not(outer))
    def _():
        relay_copy().wait_recv()
        psum[...] = (sdp[pl.ds(far, hl), 0].astype(F32) + relay[...].astype(F32)).astype(BF16)
        for i in range(hl):
            cross_copy(i).start()

    small = sgn[...]
    for k in range(1, nd):
        small_copies[k - 1].wait_recv()
        small = small + rgn[k]
    out[2 * part : 2 * part + 2, :] = small
    sums = sdp[d, 1].astype(F32)
    for k in range(1, nd):
        up_copy(k).wait_recv()
        sums = sums + rdp[k].astype(F32)
    out[part : 2 * part, :] = sums
    sums = sdp[d, 0].astype(F32)
    for k in range(1, hl):
        near_copy(k).wait_recv()
        sums = sums + rin[k].astype(F32)
    for m in range(nd // 4):
        cross_wait(m).wait_recv()
        sums = sums + rcross[m].astype(F32)
    out[0:part, :] = sums

    @pl.when(outer)
    def _():
        relay_copy().wait_send()

    @pl.when(jnp.logical_not(outer))
    def _():
        for i in range(hl):
            cross_copy(i).wait_send()

    for k in range(1, nd):
        up_copy(k).wait_send()
    for k in range(1, hl):
        near_copy(k).wait_send()
    for c in started:
        c.wait_send()


def scale_kernel(part, sums, down_out, up_out, gain_out):
    scale = 1.0 / sums[2 * part + 1 : 2 * part + 2, :]
    down_out[...] = sums[0:part, :] * scale
    up_out[...] = sums[part : 2 * part, :] * scale
    gain_out[...] = sums[2 * part : 2 * part + 1, :] * scale


def solution(mesh):
    nt, nd, ns = mesh.shape["tensor"], mesh.shape["dp"], mesh.shape["section"]
    assert ns == 2 and nd % 4 == 0

    def local(inputs, down, up, gains, head, labels, valid):
        micro, per, feats = inputs.shape
        assert micro == ns
        tokens = micro * per
        rank = down.shape[2]
        own, rows, part = tokens // ns // nt, rank // nt, rank // nd
        wire = BF16 if own % 16 == 0 and rows % 16 == 0 else F32
        vmem = pl.BlockSpec(memory_space=pltpu.VMEM)
        dma = pltpu.SemaphoreType.DMA
        anyspace = pl.BlockSpec(memory_space=pl.ANY)
        sums = pl.pallas_call(
            functools.partial(kernel, nt, nd, feats * nt),
            out_shape=jax.ShapeDtypeStruct((2 * part + 8, feats), F32),
            in_specs=[anyspace] * 7,
            out_specs=vmem,
            scratch_shapes=[
                pltpu.VMEM((tokens, feats), BF16),
                pltpu.VMEM((feats, rank), BF16),
                pltpu.VMEM((rank, feats), BF16),
                pltpu.VMEM((1, feats), BF16),
                pltpu.VMEM((feats, head.shape[1]), BF16),
                pltpu.VMEM((micro, per), jnp.int32),
                pltpu.VMEM((micro, per), jnp.int32),
                pltpu.VMEM((feats, rank), BF16),
                pltpu.VMEM((rank, feats), BF16),
                pltpu.VMEM((1, feats), BF16),
                pltpu.VMEM((2, nt, 5, own, rank), wire),
                pltpu.VMEM((2, nt, 5, own, rank), wire),
                pltpu.VMEM((nt, 3, rows, rank), wire),
                pltpu.VMEM((nt, 3, rows, rank), wire),
                pltpu.VMEM((3, rows, rank), wire),
                pltpu.VMEM((2, nt, 3, rows, rank), wire),
                pltpu.VMEM((6, own, rank), wire),
                pltpu.VMEM((2, nt, 6, own, rank), wire),
                pltpu.VMEM((nd, 2, part, feats), BF16),
                pltpu.VMEM((nd, part, feats), BF16),
                pltpu.VMEM((nd // 2, part, feats), BF16),
                pltpu.VMEM((nd // 2, part, feats), BF16),
                pltpu.VMEM((nd // 2, part, feats), BF16),
                pltpu.VMEM((nd // 4, part, feats), BF16),
                pltpu.VMEM((2, feats), F32),
                pltpu.VMEM((nd, 2, feats), F32),
                dma((7,)),
                dma((3,)), dma((3,)),
                dma((2, nt)), dma((2, nt)),
                dma((2, nt)), dma((2, nt)),
                dma((2, 2, nt)), dma((2, 2, nt)),
                dma((nt,)), dma((nt,)),
                dma((nt,)), dma((nt,)),
                dma((3, nd)), dma((3, nd)),
                dma, dma,
                dma((nd // 2,)), dma((nd // 4,)),
            ],
            compiler_params=pltpu.CompilerParams(collective_id=0, has_side_effects=True),
        )(inputs.reshape(tokens, feats), down[0], up[0], gains, head, labels, valid)
        down_t, up_g, gain_g = pl.pallas_call(
            functools.partial(scale_kernel, part),
            out_shape=(
                jax.ShapeDtypeStruct((part, feats), F32),
                jax.ShapeDtypeStruct((part, feats), F32),
                jax.ShapeDtypeStruct((1, feats), F32),
            ),
            in_specs=[vmem],
            out_specs=(vmem,) * 3,
        )(sums)
        return down_t.T[None], up_g[None], gain_g

    return jax.shard_map(
        local,
        mesh=mesh,
        in_specs=(
            P(None, "dp", "tensor"),
            P("section", "tensor", None),
            P("section", None, "tensor"),
            P("section", "tensor"),
            P("tensor", None),
            P(None, "dp"),
            P(None, "dp"),
        ),
        out_specs=(
            P("section", "tensor", "dp"),
            P("section", "dp", "tensor"),
            P("section", "tensor"),
        ),
        check_vma=False,
    )
```

profile of v0, /device:TPU:0, one launch (start us, length us, event | category | flops | bytes accessed | tf_op | source)
XLA Modules:
  0.0 35.4 jit_solution(8925564569637848816)
XLA Ops:
  0.6 33.1 %shard_map.94.sums = f32[72,1024]{1,0:T(8,128)} custom-call(bf16[256,1024]{1,0:T(8,128)(2,1)} %bitcast.7, bf16[1024,128]{1,0:T(8,128)(2,1)} %bitcast.8, bf16[128,1024]{1,0:T(8,128)(2,1)} %bitcast.9, bf16[1,1024]{1,0:T(2,128)(2,1)} %gain_hbm.1, bf16[1024,128]{1,0:T(8,128)(2,1)} %head_hbm.1, s32[2,128]{1,0:T(2,128)} %lab_hbm.1, s32[2,128]{1,0:T(2,128)} %val_hbm.1), custom_call_target="tpu_custom_call" | custom-call | tf_op jit(solution)/shard_map/pallas_call | solution.py:429
  33.8 1.7 %shard_map.95 = (f32[32,1024]{1,0:T(8,128)}, f32[32,1024]{1,0:T(8,128)}, f32[1,1024]{1,0:T(1,128)}) custom-call(f32[72,1024]{1,0:T(8,128)} %shard_map.94.sums), custom_call_target="tpu_custom_call" | custom-call | tf_op jit(solution)/shard_map/pallas_call | solution.py:474
where the time goes:
time: 35.9 us; the launch traced here: 35.4 us
  Pallas kernels  34.8 us (97%)
  between operations  0.64 us (2%)
    pallas_call x1, Pallas kernels, local(): pl.pallas_call(functools.partial(kernel, nt, nd, feats * nt), out_shape=j...  33.1 us
    pallas_call x1, Pallas kernels, local(): pl.pallas_call(functools.partial(scale_kernel, part), out_shape=(jax.Shap...  1.68 us

commit v1 on v0

--- a/solution.py
+++ b/solution.py
@@ -428,7 +428,7 @@
         anyspace = pl.BlockSpec(memory_space=pl.ANY)
         sums = pl.pallas_call(
             functools.partial(kernel, nt, nd, feats * nt),
-            out_shape=jax.ShapeDtypeStruct((2 * part + 8, feats), F32),
+            out_shape=pltpu.VMEM((2 * part + 8, feats), F32),
             in_specs=[anyspace] * 7,
             out_specs=vmem,
             scratch_shapes=[
@@ -480,7 +480,7 @@
             ),
             in_specs=[vmem],
             out_specs=(vmem,) * 3,
-        )(sums)
+        )(pltpu.with_memory_space_constraint(sums, pltpu.VMEM))
         return down_t.T[None], up_g[None], gain_g
 
     return jax.shard_map(

time: 35.9 us -> 34.2 us (0.953)
  Pallas kernels: 34.8 us -> 33.1 us
    pallas_call x1, Pallas kernels: 1.68 us -> 0.72 us  [local(): pl.pallas_call(functools.partial(scale_kernel, part), out_shape=(jax.Shap...]
    pallas_call x1, Pallas kernels: 33.1 us -> 32.4 us  [local(): pl.pallas_call(functools.partial(kernel, nt, nd, feats * nt), out_shape=p...]
where the time goes in v1:
time: 34.2 us; the launch traced here: 33.8 us
  Pallas kernels  33.1 us (97%)
  between operations  0.64 us (2%)
    pallas_call x1, Pallas kernels, local(): pl.pallas_call(functools.partial(kernel, nt, nd, feats * nt), out_shape=p...  32.4 us
    pallas_call x1, Pallas kernels, local(): pl.pallas_call(functools.partial(scale_kernel, part), out_shape=(jax.Shap...  0.72 us

profile of v1, /device:TPU:0, one launch (start us, length us, event | category | flops | bytes accessed | tf_op | source)
XLA Modules:
  0.0 33.8 jit_solution(18262452410800837278)
XLA Ops:
  0.6 32.4 %shard_map.94.sums = f32[72,1024]{1,0:T(8,128)S(1)} custom-call(bf16[256,1024]{1,0:T(8,128)(2,1)} %bitcast.7, bf16[1024,128]{1,0:T(8,128)(2,1)} %bitcast.8, bf16[128,1024]{1,0:T(8,128)(2,1)} %bitcast.9, bf16[1,1024]{1,0:T(2,128)(2,1)} %gain_hbm.1, bf16[1024,128]{1,0:T(8,128)(2,1)} %head_hbm.1, s32[2,128]{1,0:T(2,128)} %lab_hbm.1, s32[2,128]{1,0:T(2,128)} %val_hbm.1), custom_call_target="tpu_custom_call" | custom-call | tf_op jit(solution)/shard_map/pallas_call | solution.py:429
  33.1 0.7 %shard_map.95 = (f32[32,1024]{1,0:T(8,128)}, f32[32,1024]{1,0:T(8,128)}, f32[1,1024]{1,0:T(1,128)}) custom-call(f32[72,1024]{1,0:T(8,128)S(1)} %shard_map.94.sums), custom_call_target="tpu_custom_call" | custom-call | tf_op jit(solution)/shard_map/pallas_call | solution.py:474

commit v2 on v1

v2 whole, which is shorter than its diff:
```python
import functools

import jax
import jax.numpy as jnp
from jax import lax
from jax.experimental import pallas as pl
from jax.experimental.pallas import tpu as pltpu
from jax.sharding import PartitionSpec as P

MESH = pl.DeviceIdType.MESH
epsilon = 1e-05
F32 = jnp.float32
BF16 = jnp.bfloat16


def mm(a, b):
    return jnp.dot(a, b, preferred_element_type=F32)


def mm_nt(a, b):
    return lax.dot_general(a, b, (((1,), (1,)), ((), ())), preferred_element_type=F32)


def mm_tn(a, b):
    return lax.dot_general(a, b, (((0,), (0,)), ((), ())), preferred_element_type=F32)


def split(v):
    high = v.astype(BF16)
    return high, (v - high.astype(F32)).astype(BF16)


def kernel(
    nt, nd, width,
    x_hbm, dn_hbm, up_hbm, gain_hbm, head_hbm, lab_hbm, val_hbm,
    out,
    x_ref, dn_ref, up_ref, gain_ref, head_ref, lab_ref, val_ref,
    odn, oup, ogain, stok, rtok, ssq, rsq, sgram, rgram, pgram, gall, sres, res,
    sdp, rnear, rfar, relay, psum, rcross, sgn, rsm, spr, rgn,
    load, sib_s, sib_r, tok_s, tok_r, sq_s, sq_r, gr_s, gr_r, gq_s, gq_r, ga_s, ga_r, gf_s, gf_r, gc_s, gc_r,
    re_s, re_r, fw_s, fw_r, dp_s, dp_r, far_s, far_r, rel_s, rel_r, cr_s, cr_r, sm_s, sm_r, su_s, su_r,
):
    s, d, t = lax.axis_index("section"), lax.axis_index("dp"), lax.axis_index("tensor")
    first = s == 0
    tokens, feats = x_ref.shape
    rank = dn_ref.shape[1]
    half = tokens // 2
    own = half // nt
    rows = rank // nt
    part = rank // nd
    wire = stok.dtype

    hl = nd // 2
    quarter = hl // 2
    side = d // hl
    local_d = lax.rem(d, hl)
    far = (1 - side) * hl
    odd = lax.rem(d, 2)
    outer = odd == side
    deep = local_d // quarter == side
    tip = jnp.logical_and(outer, deep)
    partner = d + 1 - 2 * odd

    def ahead(k):
        return lax.rem(t + k, nt)

    def behind(k):
        return lax.rem(t + nt - k, nt)

    loads = [
        pltpu.make_async_copy(a, b, load.at[i])
        for i, (a, b) in enumerate((
            (up_hbm, up_ref), (head_hbm, head_ref), (x_hbm, x_ref), (gain_hbm, gain_ref),
            (dn_hbm, dn_ref), (lab_hbm, lab_ref), (val_hbm, val_ref),
        ))
    ]
    for c in loads:
        c.start()

    barrier = pltpu.get_barrier_semaphore()
    for k in range(1, nd):
        to = lax.rem(d + k, nd)

        @pl.when(jnp.logical_not(jnp.logical_and(tip, to == nd - 1 - d)))
        def _():
            pl.semaphore_signal(barrier, inc=1, device_id=(s, to, t), device_id_type=MESH)

    group = [(k, o) for k in range(nt) for o in (0, 1) if (k, o) != (0, 0)]
    for k, o in group:
        pl.semaphore_signal(barrier, inc=1, device_id=(1 - s if o else s, d, ahead(k)), device_id_type=MESH)

    def copy(src, dst, ss, rs, section, column):
        return pltpu.make_async_remote_copy(
            src_ref=src, dst_ref=dst, send_sem=ss, recv_sem=rs, device_id=(section, d, column), device_id_type=MESH
        )

    def put_gram(j, g):
        g = g.astype(wire)
        for i in range(nt):
            sgram[i, j] = g[i * rows : (i + 1) * rows]

    loads[0].wait()
    up = up_ref[...]
    put_gram(0, mm_nt(up, up))
    loads[1].wait()
    head = head_ref[...]
    put_gram(1, mm(up, head))

    pl.semaphore_wait(barrier, len(group) + nd - 1 - tip.astype(jnp.int32))

    def sib(i):
        a, b = ((up_ref, oup), (dn_ref, odn), (gain_ref, ogain))[i]
        return copy(a, b, sib_s.at[i], sib_r.at[i], 1 - s, t)

    def ab_scatter(k, sender):
        return copy(
            sgram.at[ahead(k), pl.ds(0, 2)], rgram.at[sender, k, pl.ds(0, 2)], gr_s.at[k], gr_r.at[sender, k], 1, ahead(k)
        )

    def cd_scatter(k):
        return copy(sgram.at[ahead(k), pl.ds(2, 2)], rgram.at[1, k, pl.ds(2, 2)], gq_s.at[k], gq_r.at[k], 1, ahead(k))

    def tok_cross(k):
        block = pl.ds(0, 2)
        return copy(
            stok.at[1 - s, ahead(k), block], rtok.at[1, k, block], tok_s.at[1, k], tok_r.at[1, k], 1 - s, ahead(k)
        )

    def tok_own(k):
        return copy(stok.at[s, ahead(k)], rtok.at[0, k], tok_s.at[0, k], tok_r.at[0, k], s, ahead(k))

    def sq_own(k):
        return copy(ssq, rsq.at[k], sq_s.at[k], sq_r.at[k], s, ahead(k))

    def ab_gather(k, section):
        block = pl.ds(0, 4)
        return copy(pgram.at[block], gall.at[t, block], ga_s.at[k], ga_r.at[k], section, ahead(k))

    def ab_forward(k):
        block = gall.at[behind(k), pl.ds(0, 4)]
        return copy(block, block, gf_s.at[k], gf_r.at[k], 0, t)

    def cd_gather(k, section):
        block = pl.ds(4, 2)
        return copy(pgram.at[block], gall.at[t, block], gc_s.at[section, k], gc_r.at[k], section, ahead(k))

    sib(0).start()
    for k in range(1, nt):
        ab_scatter(k, s).start()

    @pl.when(first)
    def _():
        ab_scatter(0, 0).start()

    for c in loads[2:]:
        c.wait()
    gain = gain_ref[...].astype(F32)
    xb = x_ref[...]
    xf = xb.astype(F32)
    xup = mm_nt(xb, up).astype(wire)
    proj = mm((xf * gain).astype(BF16), dn_ref[...]).astype(wire)
    for b in range(2):
        for i in range(nt):
            at = b * half + i * own
            stok[b, i, 0] = proj[at : at + own]
            stok[b, i, 1] = xup[at : at + own]
    for k in range(nt):
        tok_cross(k).start()

    xm = x_ref[pl.ds(pl.multiple_of(s * half, half), half), :]
    xmf = xm.astype(F32)
    xhead = mm(xm, head).astype(wire)
    for i in range(nt):
        stok[s, i, 2] = xhead[i * own : (i + 1) * own]
    ones = jnp.ones((8, feats), BF16)
    square_h, square_l = split(xmf * xmf)
    row_h, row_l = split(mm_nt(ones, square_h) + mm_nt(ones, square_l))
    ssq[0:8] = row_h.astype(wire)
    ssq[8:16] = row_l.astype(wire)

    @pl.when(s != 0)
    def _():
        sib(0).wait_recv()
        other = oup[...]
        put_gram(2, mm_nt(other, up))
        put_gram(3, mm((other.astype(F32) * gain).astype(BF16), dn_ref[...]))
        for k in range(1, nt):
            cd_scatter(k).start()

    for k in range(1, nt):
        tok_own(k).start()
        sq_own(k).start()

    @pl.when(s != 0)
    def _():
        sib(1).start()
        sib(2).start()
        ab_scatter(0, 0).wait_recv()
        mine0 = rgram[0, 0, 0:2].astype(F32)
        mine1 = sgram[t, 0:2].astype(F32)
        for k in range(1, nt):
            ab_scatter(k, 1).wait_recv()
            mine1 = mine1 + rgram[1, k, 0:2].astype(F32)
        for k in range(1, nt):
            ab_scatter(k, 0).wait_recv()
            mine0 = mine0 + rgram[0, k, 0:2].astype(F32)
        for j, v in ((0, mine0.astype(wire)), (2, mine1.astype(wire))):
            pgram[j : j + 2] = v
            gall[t, j : j + 2] = v
        for k in range(1, nt):
            ab_gather(k, 1).start()
        ab_gather(0, 0).start()
        both = sgram[t, 2:4].astype(F32)
        for k in range(1, nt):
            cd_scatter(k).wait_recv()
            both = both + rgram[1, k, 2:4].astype(F32)
        both = both.astype(wire)
        pgram[4:6] = both
        gall[t, 4:6] = both
        for k in range(1, nt):
            cd_gather(k, 1).start()
        for k in range(nt):
            cd_gather(k, 0).start()

    lab = jnp.where(first, lab_ref[0:1, :], lab_ref[1:2, :])
    val = jnp.where(first, val_ref[0:1, :], val_ref[1:2, :]).astype(F32)
    labels_n = head.shape[1]
    hot_t = jnp.where(lax.broadcasted_iota(jnp.int32, (labels_n, half), 0) == lab, val, 0.0).astype(BF16)
    val_t = jnp.broadcast_to(val, (labels_n, half)).astype(BF16)
    chosen = (
        lax.broadcasted_iota(jnp.int32, (own, half), 0) + t * own
        == lax.broadcasted_iota(jnp.int32, (own, half), 1)
    )
    pick = chosen.astype(F32).astype(BF16)
    onehot = mm_nt(pick, hot_t)
    validity = mm_nt(pick, val_t)
    count = jnp.sum(val_ref[...].astype(F32))

    mine = stok[s, t].astype(F32)
    for k in range(1, nt):
        tok_own(k).wait_recv()
        mine = mine + rtok[0, k].astype(F32)
    tok_cross(0).wait_recv()
    theirs = rtok[1, 0, 0:2].astype(F32)
    for k in range(1, nt):
        tok_cross(k).wait_recv()
        theirs = theirs + rtok[1, k, 0:2].astype(F32)
    p0 = jnp.where(first, mine[0], theirs[0])
    p1 = jnp.where(first, theirs[0], mine[0])
    v0 = jnp.where(first, mine[1], theirs[1])
    v1 = jnp.where(first, theirs[1], mine[1])
    xh = mine[2]
    sq = ssq[...].astype(F32)
    for k in range(1, nt):
        sq_own(k).wait_recv()
        sq = sq + rsq[k].astype(F32)

    def rowsum(v):
        return jnp.sum(v, axis=1, keepdims=True)

    sq0 = rowsum(jnp.where(chosen, sq[0:1] + sq[8:9], 0.0))
    inv0 = lax.rsqrt(sq0 / width + epsilon)
    pre0 = inv0 * p0
    sig0 = jax.nn.sigmoid(pre0)
    h0 = (pre0 * sig0).astype(BF16)
    h0f = h0.astype(F32)

    @pl.when(s != 0)
    def _():
        for k in range(1, nt):
            ab_gather(k, 1).wait_recv()
            ab_forward(k).start()
        for k in range(1, nt):
            cd_gather(k, 1).wait_recv()

    @pl.when(first)
    def _():
        ab_gather(0, 0).wait_recv()
        for k in range(1, nt):
            ab_forward(k).wait_recv()
        for k in range(nt):
            cd_gather(k, 0).wait_recv()

    def gram(j):
        return gall[:, j].reshape(rank, rank).astype(BF16)

    a0, b0, a1, b1, c0, d1 = (gram(j) for j in range(6))

    parts = ((0, 2), (2, 4))

    def keep(j, v):
        v = v.astype(wire)
        sres[j] = v
        res[s, t, j] = v

    def shared(m, k, sender):
        at, size = parts[m]
        span = pl.ds(at, size)
        return copy(
            sres.at[span], res.at[sender, t, span], re_s.at[m, k], re_r.at[m, sender, k], 1 if k else 1 - sender, ahead(k)
        )

    def onward(m, k, sender):
        at, size = parts[m]
        block = res.at[sender, behind(k), pl.ds(at, size)]
        return copy(block, block, fw_s.at[m, sender, k], fw_r.at[m, sender, k], 0, t)

    def share(m):
        for k in list(range(1, nt)) + [0]:
            shared(m, k, s).start()

    h0a = mm(h0, a0)
    p1 = p1 + mm(h0, d1)
    s1u0 = v0 + h0a
    s1u1 = v1 + mm(h0, c0)
    base = xh + mm(h0, b0)
    sq1 = sq0 + rowsum(h0f * (v0 + s1u0))
    inv1 = lax.rsqrt(sq1 / width + epsilon)
    pre1 = inv1 * p1
    sig1 = jax.nn.sigmoid(pre1)
    h1 = (pre1 * sig1).astype(BF16)
    h1f = h1.astype(F32)
    keep(0, h0)
    keep(1, h1)
    share(0)
    yu1 = s1u1 + mm(h1, a1)
    yu0 = s1u0 + mm_nt(h1, c0)
    base = base + mm(h1, b1)
    sq2 = sq1 + rowsum(h1f * (s1u1 + yu1))
    inv2 = lax.rsqrt(sq2 / width + epsilon)
    logits = inv2 * base
    expo = jnp.exp(logits - jnp.max(logits, axis=1, keepdims=True))
    cot = expo / rowsum(expo) * validity - onehot
    radial = rowsum(cot * base)
    wh = (inv2 * cot).astype(BF16)
    keep(2, wh)
    ch = inv2 * inv2 * inv2 / width * radial
    hg1 = mm_nt(wh, b1) - ch * yu1
    act1 = hg1 * sig1 * (1.0 + pre1 * (1.0 - sig1))
    w1 = (inv1 * act1).astype(BF16)
    c1 = inv1 * inv1 * inv1 / width * rowsum(act1 * p1)
    ch_h, ch_l = split(ch)
    c1_h, c1_l = split(c1)
    lane = lax.broadcasted_iota(jnp.int32, (own, rank), 1)
    q4 = rank // 4
    keep(3, w1)
    keep(4, jnp.where(
        lane < q4, ch_h.astype(F32),
        jnp.where(lane < 2 * q4, ch_l.astype(F32), jnp.where(lane < 3 * q4, c1_h.astype(F32), c1_l.astype(F32))),
    ))
    hg0 = mm_nt(wh, b0) - ch * yu0 + mm_nt(w1, d1) - c1 * s1u0
    act0 = hg0 * sig0 * (1.0 + pre0 * (1.0 - sig0))
    w0 = (inv0 * act0).astype(BF16)
    keep(5, w0)
    share(1)

    def got(j):
        return res[:, :, j].reshape(tokens, res.shape[-1])

    def piece(j, full):
        full = full.astype(BF16)
        for i in range(nd):
            sdp[i, j] = full[i * part : (i + 1) * part]

    near_far = far + side * quarter
    deep_far = far + (1 - side) * quarter

    def remote(src, dst, ss, rs, to):
        return pltpu.make_async_remote_copy(
            src_ref=src, dst_ref=dst, send_sem=ss, recv_sem=rs, device_id=(s, to, t), device_id_type=MESH
        )

    def near_copy(k, j):
        to = side * hl + lax.rem(local_d + k, hl)
        return remote(sdp.at[to, j], rnear.at[j, k], dp_s.at[j, k], dp_r.at[j, k], to)

    def up_copy(i):
        return remote(sdp.at[near_far + i, 1], rfar.at[local_d], far_s.at[i], far_r.at[local_d], near_far + i)

    def up_wait(m):
        return remote(sdp.at[far, 1], rfar.at[m], far_s.at[0], far_r.at[m], far)

    def relay_copy(g):
        block = pl.ds(near_far if g == 2 else deep_far, quarter)
        return remote(sdp.at[block, 1 if g == 1 else 0], relay.at[g], rel_s.at[g], rel_r.at[g], partner)

    def cross_copy(g, i):
        m = local_d // 2
        to = (near_far if g == 2 else deep_far) + i
        return remote(psum.at[g, i], rcross.at[1 if g == 1 else 0, m], cr_s.at[g, i], cr_r.at[1 if g == 1 else 0, m], to)

    def cross_wait(j, m):
        return remote(psum.at[0, 0], rcross.at[j, m], cr_s.at[0, 0], cr_r.at[j, m], near_far)

    def small_copy(k):
        return remote(spr, rgn.at[d // 2], sm_s.at[k], sm_r.at[d // 2], lax.rem(d + k, nd))

    def small_wait(p):
        return remote(spr, rgn.at[p], sm_s.at[1], sm_r.at[p], partner)

    def small_first():
        return remote(sgn, rsm, su_s, su_r, partner)

    def tail(sec):
        u0, u1 = (oup, up_ref) if sec else (up_ref, oup)
        senders = [(k, b) for k in range(1, nt) for b in (1, 0)]

        def collect(m):
            if sec:
                for k, b in senders:
                    shared(m, k, b).wait_recv()
                    onward(m, k, b).start()
                shared(m, 0, 0).wait_recv()
            else:
                shared(m, 0, 1).wait_recv()
                for k, b in senders:
                    onward(m, k, b).wait_recv()

        if sec == 0:
            for i in range(3):
                sib(i).wait_recv()
        collect(0)
        h0g, h1g = got(0).astype(BF16), got(1).astype(BF16)
        s1 = xf + mm(h0g, u0[...])
        y = s1 + mm(h1g, u1[...])
        collect(1)
        w1g = got(3).astype(BF16)
        state, own_w = (s1, w1g) if sec else (xf, got(5).astype(BF16))
        piece(0, mm_tn(own_w, (state * gain).astype(BF16)))

        @pl.when(outer)
        def _():
            relay_copy(0).start()

        @pl.when(jnp.logical_not(outer))
        def _():
            for k in range(1, hl):
                near_copy(k, 0).start()

        cg = got(4).astype(F32)
        chg = cg[:, 0:1] + cg[:, q4 : q4 + 1]
        g = mm_nt(got(2).astype(BF16), head_ref[...]) - chg * y
        if sec == 0:
            c1g = cg[:, 2 * q4 : 2 * q4 + 1] + cg[:, 3 * q4 : 3 * q4 + 1]
            g = g + ogain[...].astype(F32) * mm_nt(w1g, odn[...]) - c1g * s1
        piece(1, mm_tn(h1g if sec else h0g, g.astype(BF16)))
        gain_row = jnp.sum(mm_nt(own_w, dn_ref[...]) * state, axis=0, keepdims=True)
        sgn[0:1, :] = gain_row
        sgn[1:2, :] = jnp.full((1, feats), count, F32)

    @pl.when(first)
    def _():
        tail(0)

    @pl.when(s != 0)
    def _():
        tail(1)

    @pl.when(outer)
    def _():
        small_first().start()
        queue = [relay_copy(0), relay_copy(1), relay_copy(2)]
        queue += [up_copy(i) for i in range(quarter)]
        queue += [near_copy(k, j) for j in (1, 0) for k in range(1, hl)]
        for i in range(1, len(queue)):
            if i >= 2:
                queue[i - 2].wait_send()
            queue[i].start()
        for c in queue[max(0, len(queue) - 2):]:
            c.wait_send()

    @pl.when(jnp.logical_not(outer))
    def _():
        for i in range(quarter):
            up_copy(i).start()
        for k in range(1, hl):
            near_copy(k, 1).start()
        small_first().wait_recv()
        spr[...] = sgn[...] + rsm[...]
        for k in range(1, nd):
            small_copy(k).start()
        for g in range(3):
            relay_copy(g).wait_recv()
            for i in range(quarter):
                at = (near_far if g == 2 else deep_far) + i
                psum[g, i] = (sdp[at, 1 if g == 1 else 0].astype(F32) + relay[g, i].astype(F32)).astype(BF16)
                cross_copy(g, i).start()

    rgn_own = d // 2

    @pl.when(outer)
    def _():
        small_wait(rgn_own).wait_recv()
        spr[...] = rgn[rgn_own]

    small = spr[...]
    for j in range(1, nd // 2):
        p = lax.rem(rgn_own + j, nd // 2)
        small_wait(p).wait_recv()
        small = small + rgn[p]
    out[2 * part : 2 * part + 2, :] = small

    def total(j, from_pairs):
        sums = sdp[d, j].astype(F32)
        for k in range(1, hl):
            near_copy(k, j).wait_recv()
            sums = sums + rnear[j, k].astype(F32)
        if from_pairs:
            for m in range(nd // 4):
                cross_wait(j, m).wait_recv()
                sums = sums + rcross[j, m].astype(F32)
        else:
            for m in range(hl):
                up_wait(m).wait_recv()
                sums = sums + rfar[m].astype(F32)
        out[j * part : (j + 1) * part, :] = sums

    @pl.when(deep)
    def _():
        total(1, True)

    @pl.when(jnp.logical_not(deep))
    def _():
        total(1, False)

    total(0, True)

    @pl.when(outer)
    def _():
        small_first().wait_send()

    @pl.when(jnp.logical_not(outer))
    def _():
        for i in range(quarter):
            up_copy(i).wait_send()
            for g in range(3):
                cross_copy(g, i).wait_send()
        for k in range(1, hl):
            near_copy(k, 1).wait_send()
        for k in range(1, nd):
            small_copy(k).wait_send()
        for k in range(1, hl):
            near_copy(k, 0).wait_send()

    sib(0).wait_send()
    for k in range(1, nt):
        ab_scatter(k, s).wait_send()
        tok_own(k).wait_send()
        sq_own(k).wait_send()
    for k in range(nt):
        tok_cross(k).wait_send()
        for m in range(2):
            shared(m, k, s).wait_send()

    @pl.when(first)
    def _():
        ab_scatter(0, 0).wait_send()

    @pl.when(s != 0)
    def _():
        sib(1).wait_send()
        sib(2).wait_send()
        ab_gather(0, 0).wait_send()
        cd_gather(0, 0).wait_send()
        for k in range(1, nt):
            cd_scatter(k).wait_send()
            ab_gather(k, 1).wait_send()
            ab_forward(k).wait_send()
            cd_gather(k, 0).wait_send()
            cd_gather(k, 1).wait_send()
            for m in range(2):
                for b in range(2):
                    onward(m, k, b).wait_send()


def scale_kernel(part, sums, down_out, up_out, gain_out):
    scale = 1.0 / sums[2 * part + 1 : 2 * part + 2, :]
    down_out[...] = sums[0:part, :] * scale
    up_out[...] = sums[part : 2 * part, :] * scale
    gain_out[...] = sums[2 * part : 2 * part + 1, :] * scale


def solution(mesh):
    nt, nd, ns = mesh.shape["tensor"], mesh.shape["dp"], mesh.shape["section"]
    assert ns == 2 and nd % 4 == 0

    def local(inputs, down, up, gains, head, labels, valid):
        micro, per, feats = inputs.shape
        assert micro == ns
        tokens = micro * per
        rank = down.shape[2]
        own, rows, part = tokens // ns // nt, rank // nt, rank // nd
        wire = BF16 if own % 16 == 0 and rows % 16 == 0 else F32
        vmem = pl.BlockSpec(memory_space=pltpu.VMEM)
        dma = pltpu.SemaphoreType.DMA
        anyspace = pl.BlockSpec(memory_space=pl.ANY)
        sums = pl.pallas_call(
            functools.partial(kernel, nt, nd, feats * nt),
            out_shape=pltpu.VMEM((2 * part + 8, feats), F32),
            in_specs=[anyspace] * 7,
            out_specs=vmem,
            scratch_shapes=[
                pltpu.VMEM((tokens, feats), BF16),
                pltpu.VMEM((feats, rank), BF16),
                pltpu.VMEM((rank, feats), BF16),
                pltpu.VMEM((1, feats), BF16),
                pltpu.VMEM((feats, head.shape[1]), BF16),
                pltpu.VMEM((micro, per), jnp.int32),
                pltpu.VMEM((micro, per), jnp.int32),
                pltpu.VMEM((feats, rank), BF16),
                pltpu.VMEM((rank, feats), BF16),
                pltpu.VMEM((1, feats), BF16),
                pltpu.VMEM((2, nt, 3, own, rank), wire),
                pltpu.VMEM((2, nt, 3, own, rank), wire),
                pltpu.VMEM((16, tokens // 2), wire),
                pltpu.VMEM((nt, 16, tokens // 2), wire),
                pltpu.VMEM((nt, 4, rows, rank), wire),
                pltpu.VMEM((2, nt, 4, rows, rank), wire),
                pltpu.VMEM((6, rows, rank), wire),
                pltpu.VMEM((nt, 6, rows, rank), wire),
                pltpu.VMEM((6, own, rank), wire),
                pltpu.VMEM((2, nt, 6, own, rank), wire),
                pltpu.VMEM((nd, 2, part, feats), BF16),
                pltpu.VMEM((2, nd // 2, part, feats), BF16),
                pltpu.VMEM((nd // 2, part, feats), BF16),
                pltpu.VMEM((3, nd // 4, part, feats), BF16),
                pltpu.VMEM((3, nd // 4, part, feats), BF16),
                pltpu.VMEM((2, nd // 4, part, feats), BF16),
                pltpu.VMEM((2, feats), F32),
                pltpu.VMEM((2, feats), F32),
                pltpu.VMEM((2, feats), F32),
                pltpu.VMEM((nd // 2, 2, feats), F32),
                dma((7,)),
                dma((3,)), dma((3,)),
                dma((2, nt)), dma((2, nt)),
                dma((nt,)), dma((nt,)),
                dma((nt,)), dma((2, nt)),
                dma((nt,)), dma((nt,)),
                dma((nt,)), dma((nt,)),
                dma((nt,)), dma((nt,)),
                dma((2, nt)), dma((nt,)),
                dma((2, nt)), dma((2, 2, nt)),
                dma((2, 2, nt)), dma((2, 2, nt)),
                dma((2, nd // 2)), dma((2, nd // 2)),
                dma((nd // 4,)), dma((nd // 2,)),
                dma((3,)), dma((3,)),
                dma((3, nd // 4)), dma((2, nd // 4)),
                dma((nd,)), dma((nd // 2,)),
                dma, dma,
            ],
            compiler_params=pltpu.CompilerParams(collective_id=0, has_side_effects=True),
        )(inputs.reshape(tokens, feats), down[0], up[0], gains, head, labels, valid)
        down_t, up_g, gain_g = pl.pallas_call(
            functools.partial(scale_kernel, part),
            out_shape=(
                jax.ShapeDtypeStruct((part, feats), F32),
                jax.ShapeDtypeStruct((part, feats), F32),
                jax.ShapeDtypeStruct((1, feats), F32),
            ),
            in_specs=[vmem],
            out_specs=(vmem,) * 3,
        )(pltpu.with_memory_space_constraint(sums, pltpu.VMEM))
        return down_t.T[None], up_g[None], gain_g

    return jax.shard_map(
        local,
        mesh=mesh,
        in_specs=(
            P(None, "dp", "tensor"),
            P("section", "tensor", None),
            P("section", None, "tensor"),
            P("section", "tensor"),
            P("tensor", None),
            P(None, "dp"),
            P(None, "dp"),
        ),
        out_specs=(
            P("section", "tensor", "dp"),
            P("section", "dp", "tensor"),
            P("section", "tensor"),
        ),
        check_vma=False,
    )
```

time: 34.2 us -> 31.2 us (0.912)
  Pallas kernels: 33.1 us -> 30.4 us
    pallas_call x1, Pallas kernels: 32.4 us -> 29.7 us  [local(): pl.pallas_call(functools.partial(kernel, nt, nd, feats * nt), out_shape=p...]
where the time goes in v2:
time: 31.2 us; the launch traced here: 31 us
  Pallas kernels  30.4 us (97%)
  between operations  0.64 us (2%)
    pallas_call x1, Pallas kernels, local(): pl.pallas_call(functools.partial(kernel, nt, nd, feats * nt), out_shape=p...  29.7 us
    pallas_call x1, Pallas kernels, local(): pl.pallas_call(functools.partial(scale_kernel, part), out_shape=(jax.Shap...  0.72 us

profile of v2, /device:TPU:0, one launch (start us, length us, event | category | flops | bytes accessed | tf_op | source)
XLA Modules:
  0.0 31.0 jit_solution(15657663477452024668)
XLA Ops:
  0.6 29.7 %shard_map.94.sums = f32[72,1024]{1,0:T(8,128)S(1)} custom-call(bf16[256,1024]{1,0:T(8,128)(2,1)} %bitcast.7, bf16[1024,128]{1,0:T(8,128)(2,1)} %bitcast.8, bf16[128,1024]{1,0:T(8,128)(2,1)} %bitcast.9, bf16[1,1024]{1,0:T(2,128)(2,1)} %gain_hbm.1, bf16[1024,128]{1,0:T(8,128)(2,1)} %head_hbm.1, s32[2,128]{1,0:T(2,128)} %lab_hbm.1, s32[2,128]{1,0:T(2,128)} %val_hbm.1), custom_call_target="tpu_custom_call" | custom-call | tf_op jit(solution)/shard_map/pallas_call | solution.py:597
  30.3 0.7 %shard_map.95 = (f32[32,1024]{1,0:T(8,128)}, f32[32,1024]{1,0:T(8,128)}, f32[1,1024]{1,0:T(1,128)}) custom-call(f32[72,1024]{1,0:T(8,128)S(1)} %shard_map.94.sums), custom_call_target="tpu_custom_call" | custom-call | tf_op jit(solution)/shard_map/pallas_call | solution.py:653

commit v3 on v2

--- a/solution.py
+++ b/solution.py
@@ -94,6 +94,15 @@
             src_ref=src, dst_ref=dst, send_sem=ss, recv_sem=rs, device_id=(section, d, column), device_id_type=MESH
         )
 
+    def whole(ref, sem):
+        return copy(ref, ref, sem, sem, 1 - s, t)
+
+    def arrived(ref, sem):
+        whole(ref, sem).wait_recv()
+
+    def sent(ref, sem):
+        whole(ref, sem).wait_send()
+
     def put_gram(j, g):
         g = g.astype(wire)
         for i in range(nt):
@@ -114,35 +123,37 @@
 
     def ab_scatter(k, sender):
         return copy(
-            sgram.at[ahead(k), pl.ds(0, 2)], rgram.at[sender, k, pl.ds(0, 2)], gr_s.at[k], gr_r.at[sender, k], 1, ahead(k)
+            sgram.at[ahead(k), pl.ds(0, 2)], rgram.at[sender, k, pl.ds(0, 2)], gr_s, gr_r.at[sender], 1, ahead(k)
         )
 
     def cd_scatter(k):
-        return copy(sgram.at[ahead(k), pl.ds(2, 2)], rgram.at[1, k, pl.ds(2, 2)], gq_s.at[k], gq_r.at[k], 1, ahead(k))
+        return copy(sgram.at[ahead(k), pl.ds(2, 2)], rgram.at[1, k, pl.ds(2, 2)], gq_s, gq_r, 1, ahead(k))
 
     def tok_cross(k):
         block = pl.ds(0, 2)
         return copy(
-            stok.at[1 - s, ahead(k), block], rtok.at[1, k, block], tok_s.at[1, k], tok_r.at[1, k], 1 - s, ahead(k)
+            stok.at[1 - s, ahead(k), block], rtok.at[1, k, block], tok_s.at[1], tok_r.at[1], 1 - s, ahead(k)
         )
 
     def tok_own(k):
-        return copy(stok.at[s, ahead(k)], rtok.at[0, k], tok_s.at[0, k], tok_r.at[0, k], s, ahead(k))
+        return copy(stok.at[s, ahead(k)], rtok.at[0, k], tok_s.at[0], tok_r.at[0], s, ahead(k))
 
     def sq_own(k):
-        return copy(ssq, rsq.at[k], sq_s.at[k], sq_r.at[k], s, ahead(k))
-
-    def ab_gather(k, section):
+        return copy(ssq, rsq.at[k], sq_s, sq_r, s, ahead(k))
+
+    ab_all = gall.at[:, pl.ds(0, 4)]
+    cd_all = gall.at[:, pl.ds(4, 2)]
+
+    def ab_gather(k):
         block = pl.ds(0, 4)
-        return copy(pgram.at[block], gall.at[t, block], ga_s.at[k], ga_r.at[k], section, ahead(k))
-
-    def ab_forward(k):
-        block = gall.at[behind(k), pl.ds(0, 4)]
-        return copy(block, block, gf_s.at[k], gf_r.at[k], 0, t)
+        return copy(pgram.at[block], gall.at[t, block], ga_s, ga_r, 1, ahead(k))
+
+    def ab_forward():
+        return copy(ab_all, ab_all, gf_s, gf_r, 0, t)
 
     def cd_gather(k, section):
         block = pl.ds(4, 2)
-        return copy(pgram.at[block], gall.at[t, block], gc_s.at[section, k], gc_r.at[k], section, ahead(k))
+        return copy(pgram.at[block], gall.at[t, block], gc_s.at[section], gc_r, section, ahead(k))
 
     sib(0).start()
     for k in range(1, nt):
@@ -195,24 +206,22 @@
     def _():
         sib(1).start()
         sib(2).start()
-        ab_scatter(0, 0).wait_recv()
-        mine0 = rgram[0, 0, 0:2].astype(F32)
+        arrived(rgram.at[1, pl.ds(1, nt - 1), pl.ds(0, 2)], gr_r.at[1])
         mine1 = sgram[t, 0:2].astype(F32)
         for k in range(1, nt):
-            ab_scatter(k, 1).wait_recv()
             mine1 = mine1 + rgram[1, k, 0:2].astype(F32)
+        arrived(rgram.at[0, :, pl.ds(0, 2)], gr_r.at[0])
+        mine0 = rgram[0, 0, 0:2].astype(F32)
         for k in range(1, nt):
-            ab_scatter(k, 0).wait_recv()
             mine0 = mine0 + rgram[0, k, 0:2].astype(F32)
         for j, v in ((0, mine0.astype(wire)), (2, mine1.astype(wire))):
             pgram[j : j + 2] = v
             gall[t, j : j + 2] = v
         for k in range(1, nt):
-            ab_gather(k, 1).start()
-        ab_gather(0, 0).start()
+            ab_gather(k).start()
+        arrived(rgram.at[1, pl.ds(1, nt - 1), pl.ds(2, 2)], gq_r)
         both = sgram[t, 2:4].astype(F32)
         for k in range(1, nt):
-            cd_scatter(k).wait_recv()
             both = both + rgram[1, k, 2:4].astype(F32)
         both = both.astype(wire)
         pgram[4:6] = both
@@ -236,23 +245,22 @@
     validity = mm_nt(pick, val_t)
     count = jnp.sum(val_ref[...].astype(F32))
 
+    arrived(rtok.at[0, pl.ds(1, nt - 1)], tok_r.at[0])
     mine = stok[s, t].astype(F32)
     for k in range(1, nt):
-        tok_own(k).wait_recv()
         mine = mine + rtok[0, k].astype(F32)
-    tok_cross(0).wait_recv()
+    arrived(rtok.at[1, :, pl.ds(0, 2)], tok_r.at[1])
     theirs = rtok[1, 0, 0:2].astype(F32)
     for k in range(1, nt):
-        tok_cross(k).wait_recv()
         theirs = theirs + rtok[1, k, 0:2].astype(F32)
     p0 = jnp.where(first, mine[0], theirs[0])
     p1 = jnp.where(first, theirs[0], mine[0])
     v0 = jnp.where(first, mine[1], theirs[1])
     v1 = jnp.where(first, theirs[1], mine[1])
     xh = mine[2]
+    arrived(rsq.at[pl.ds(1, nt - 1)], sq_r)
     sq = ssq[...].astype(F32)
     for k in range(1, nt):
-        sq_own(k).wait_recv()
         sq = sq + rsq[k].astype(F32)
 
     def rowsum(v):
@@ -267,19 +275,14 @@
 
     @pl.when(s != 0)
     def _():
-        for k in range(1, nt):
-            ab_gather(k, 1).wait_recv()
-            ab_forward(k).start()
-        for k in range(1, nt):
-            cd_gather(k, 1).wait_recv()
+        arrived(gall.at[pl.ds(1, nt - 1), pl.ds(0, 4)], ga_r)
+        ab_forward().start()
+        arrived(gall.at[pl.ds(1, nt - 1), pl.ds(4, 2)], gc_r)
 
     @pl.when(first)
     def _():
-        ab_gather(0, 0).wait_recv()
-        for k in range(1, nt):
-            ab_forward(k).wait_recv()
-        for k in range(nt):
-            cd_gather(k, 0).wait_recv()
+        ab_forward().wait_recv()
+        arrived(cd_all, gc_r)
 
     def gram(j):
         return gall[:, j].reshape(rank, rank).astype(BF16)
@@ -293,21 +296,23 @@
         sres[j] = v
         res[s, t, j] = v
 
-    def shared(m, k, sender):
+    def shared(m, k):
         at, size = parts[m]
         span = pl.ds(at, size)
-        return copy(
-            sres.at[span], res.at[sender, t, span], re_s.at[m, k], re_r.at[m, sender, k], 1 if k else 1 - sender, ahead(k)
-        )
-
-    def onward(m, k, sender):
+        return copy(sres.at[span], res.at[s, t, span], re_s.at[m], re_r.at[m, s], 1, ahead(k))
+
+    def onward(m, b):
         at, size = parts[m]
-        block = res.at[sender, behind(k), pl.ds(at, size)]
-        return copy(block, block, fw_s.at[m, sender, k], fw_r.at[m, sender, k], 0, t)
+        block = res.at[b, :, pl.ds(at, size)]
+        return copy(block, block, fw_s.at[m], fw_r.at[m], 0, t)
 
     def share(m):
-        for k in list(range(1, nt)) + [0]:
-            shared(m, k, s).start()
+        for k in range(1, nt):
+            shared(m, k).start()
+
+        @pl.when(first)
+        def _():
+            shared(m, 0).start()
 
     h0a = mm(h0, a0)
     p1 = p1 + mm(h0, d1)
@@ -372,13 +377,10 @@
 
     def near_copy(k, j):
         to = side * hl + lax.rem(local_d + k, hl)
-        return remote(sdp.at[to, j], rnear.at[j, k], dp_s.at[j, k], dp_r.at[j, k], to)
+        return remote(sdp.at[to, j], rnear.at[j, k], dp_s.at[j, k - 1], dp_r.at[j], to)
 
     def up_copy(i):
-        return remote(sdp.at[near_far + i, 1], rfar.at[local_d], far_s.at[i], far_r.at[local_d], near_far + i)
-
-    def up_wait(m):
-        return remote(sdp.at[far, 1], rfar.at[m], far_s.at[0], far_r.at[m], far)
+        return remote(sdp.at[near_far + i, 1], rfar.at[local_d], far_s.at[i], far_r, near_far + i)
 
     def relay_copy(g):
         block = pl.ds(near_far if g == 2 else deep_far, quarter)
@@ -387,34 +389,28 @@
     def cross_copy(g, i):
         m = local_d // 2
         to = (near_far if g == 2 else deep_far) + i
-        return remote(psum.at[g, i], rcross.at[1 if g == 1 else 0, m], cr_s.at[g, i], cr_r.at[1 if g == 1 else 0, m], to)
-
-    def cross_wait(j, m):
-        return remote(psum.at[0, 0], rcross.at[j, m], cr_s.at[0, 0], cr_r.at[j, m], near_far)
+        return remote(psum.at[g, i], rcross.at[1 if g == 1 else 0, m], cr_s, cr_r.at[1 if g == 1 else 0], to)
 
     def small_copy(k):
-        return remote(spr, rgn.at[d // 2], sm_s.at[k], sm_r.at[d // 2], lax.rem(d + k, nd))
-
-    def small_wait(p):
-        return remote(spr, rgn.at[p], sm_s.at[1], sm_r.at[p], partner)
+        to = lax.rem(d + k, nd)
+        return remote(spr, rgn.at[d // 2], sm_s, sm_r.at[(to // 2 != d // 2).astype(jnp.int32)], to)
 
     def small_first():
         return remote(sgn, rsm, su_s, su_r, partner)
 
     def tail(sec):
         u0, u1 = (oup, up_ref) if sec else (up_ref, oup)
-        senders = [(k, b) for k in range(1, nt) for b in (1, 0)]
 
         def collect(m):
+            at, size = parts[m]
+            span = pl.ds(at, size)
             if sec:
-                for k, b in senders:
-                    shared(m, k, b).wait_recv()
-                    onward(m, k, b).start()
-                shared(m, 0, 0).wait_recv()
+                arrived(res.at[1, pl.ds(1, nt - 1), span], re_r.at[m, 1])
+                onward(m, 1).start()
+                arrived(res.at[0, :, span], re_r.at[m, 0])
+                onward(m, 0).start()
             else:
-                shared(m, 0, 1).wait_recv()
-                for k, b in senders:
-                    onward(m, k, b).wait_recv()
+                arrived(res.at[:, :, span], fw_r.at[m])
 
         if sec == 0:
             for i in range(3):
@@ -490,28 +486,28 @@
 
     @pl.when(outer)
     def _():
-        small_wait(rgn_own).wait_recv()
+        arrived(rgn.at[rgn_own], sm_r.at[0])
         spr[...] = rgn[rgn_own]
 
+    arrived(rgn.at[pl.ds(1, nd // 2 - 1)], sm_r.at[1])
     small = spr[...]
     for j in range(1, nd // 2):
         p = lax.rem(rgn_own + j, nd // 2)
-        small_wait(p).wait_recv()
         small = small + rgn[p]
     out[2 * part : 2 * part + 2, :] = small
 
     def total(j, from_pairs):
+        arrived(rnear.at[j, pl.ds(1, hl - 1)], dp_r.at[j])
         sums = sdp[d, j].astype(F32)
         for k in range(1, hl):
-            near_copy(k, j).wait_recv()
             sums = sums + rnear[j, k].astype(F32)
         if from_pairs:
+            arrived(rcross.at[j], cr_r.at[j])
             for m in range(nd // 4):
-                cross_wait(j, m).wait_recv()
                 sums = sums + rcross[j, m].astype(F32)
         else:
+            arrived(rfar, far_r)
             for m in range(hl):
-                up_wait(m).wait_recv()
                 sums = sums + rfar[m].astype(F32)
         out[j * part : (j + 1) * part, :] = sums
 
@@ -533,44 +529,36 @@
     def _():
         for i in range(quarter):
             up_copy(i).wait_send()
-            for g in range(3):
-                cross_copy(g, i).wait_send()
+        sent(psum, cr_s)
         for k in range(1, hl):
             near_copy(k, 1).wait_send()
-        for k in range(1, nd):
-            small_copy(k).wait_send()
-        for k in range(1, hl):
             near_copy(k, 0).wait_send()
+        sent(rgn.at[pl.ds(1, nd - 1)], sm_s)
 
     sib(0).wait_send()
-    for k in range(1, nt):
-        ab_scatter(k, s).wait_send()
-        tok_own(k).wait_send()
-        sq_own(k).wait_send()
-    for k in range(nt):
-        tok_cross(k).wait_send()
-        for m in range(2):
-            shared(m, k, s).wait_send()
+    sent(rtok.at[0, pl.ds(1, nt - 1)], tok_s.at[0])
+    sent(rtok.at[1, :, pl.ds(0, 2)], tok_s.at[1])
+    sent(rsq.at[pl.ds(1, nt - 1)], sq_s)
 
     @pl.when(first)
     def _():
-        ab_scatter(0, 0).wait_send()
+        sent(rgram.at[0, :, pl.ds(0, 2)], gr_s)
+        for m, (at, size) in enumerate(parts):
+            sent(res.at[0, :, pl.ds(at, size)], re_s.at[m])
 
     @pl.when(s != 0)
     def _():
         sib(1).wait_send()
         sib(2).wait_send()
-        ab_gather(0, 0).wait_send()
-        cd_gather(0, 0).wait_send()
-        for k in range(1, nt):
-            cd_scatter(k).wait_send()
-            ab_gather(k, 1).wait_send()
-            ab_forward(k).wait_send()
-            cd_gather(k, 0).wait_send()
-            cd_gather(k, 1).wait_send()
-            for m in range(2):
-                for b in range(2):
-                    onward(m, k, b).wait_send()
+        sent(rgram.at[1, pl.ds(1, nt - 1), pl.ds(0, 2)], gr_s)
+        sent(rgram.at[1, pl.ds(1, nt - 1), pl.ds(2, 2)], gq_s)
+        sent(gall.at[pl.ds(1, nt - 1), pl.ds(0, 4)], ga_s)
+        ab_forward().wait_send()
+        sent(cd_all, gc_s.at[0])
+        sent(gall.at[pl.ds(1, nt - 1), pl.ds(4, 2)], gc_s.at[1])
+        for m, (at, size) in enumerate(parts):
+            sent(res.at[1, pl.ds(1, nt - 1), pl.ds(at, size)], re_s.at[m])
+            sent(res.at[:, :, pl.ds(at, size)], fw_s.at[m])
 
 
 def scale_kernel(part, sums, down_out, up_out, gain_out):
@@ -629,23 +617,23 @@
                 pltpu.VMEM((2, feats), F32),
                 pltpu.VMEM((2, feats), F32),
                 pltpu.VMEM((2, feats), F32),
-                pltpu.VMEM((nd // 2, 2, feats), F32),
+                pltpu.VMEM((nd, 2, feats), F32),
                 dma((7,)),
                 dma((3,)), dma((3,)),
-                dma((2, nt)), dma((2, nt)),
-                dma((nt,)), dma((nt,)),
-                dma((nt,)), dma((2, nt)),
-                dma((nt,)), dma((nt,)),
-                dma((nt,)), dma((nt,)),
-                dma((nt,)), dma((nt,)),
-                dma((2, nt)), dma((nt,)),
-                dma((2, nt)), dma((2, 2, nt)),
-                dma((2, 2, nt)), dma((2, 2, nt)),
-                dma((2, nd // 2)), dma((2, nd // 2)),
-                dma((nd // 4,)), dma((nd // 2,)),
+                dma((2,)), dma((2,)),
+                dma, dma,
+                dma, dma((2,)),
+                dma, dma,
+                dma, dma,
+                dma, dma,
+                dma((2,)), dma,
+                dma((2,)), dma((2, 2)),
+                dma((2,)), dma((2,)),
+                dma((2, nd // 2 - 1)), dma((2,)),
+                dma((nd // 4,)), dma,
                 dma((3,)), dma((3,)),
-                dma((3, nd // 4)), dma((2, nd // 4)),
-                dma((nd,)), dma((nd // 2,)),
+                dma, dma((2,)),
+                dma, dma((2,)),
                 dma, dma,
             ],
             compiler_params=pltpu.CompilerParams(collective_id=0, has_side_effects=True),

time: 31.2 us -> 30.1 us (0.965)
  Pallas kernels: 30.4 us -> 29.3 us
    pallas_call x1, Pallas kernels: 29.7 us -> 28.6 us  [local(): pl.pallas_call(functools.partial(kernel, nt, nd, feats * nt), out_shape=p...]
where the time goes in v3:
time: 30.1 us; the launch traced here: 30 us
  Pallas kernels  29.3 us (97%)
  between operations  0.64 us (2%)
    pallas_call x1, Pallas kernels, local(): pl.pallas_call(functools.partial(kernel, nt, nd, feats * nt), out_shape=p...  28.6 us
    pallas_call x1, Pallas kernels, local(): pl.pallas_call(functools.partial(scale_kernel, part), out_shape=(jax.Shap...  0.72 us

profile of v3, /device:TPU:0, one launch (start us, length us, event | category | flops | bytes accessed | tf_op | source)
XLA Modules:
  0.0 30.0 jit_solution(9890580753415629452)
XLA Ops:
  0.6 28.6 %shard_map.94.sums = f32[72,1024]{1,0:T(8,128)S(1)} custom-call(bf16[256,1024]{1,0:T(8,128)(2,1)} %bitcast.7, bf16[1024,128]{1,0:T(8,128)(2,1)} %bitcast.8, bf16[128,1024]{1,0:T(8,128)(2,1)} %bitcast.9, bf16[1,1024]{1,0:T(2,128)(2,1)} %gain_hbm.1, bf16[1024,128]{1,0:T(8,128)(2,1)} %head_hbm.1, s32[2,128]{1,0:T(2,128)} %lab_hbm.1, s32[2,128]{1,0:T(2,128)} %val_hbm.1), custom_call_target="tpu_custom_call" | custom-call | tf_op jit(solution)/shard_map/pallas_call | solution.py:585
  29.3 0.7 %shard_map.95 = (f32[32,1024]{1,0:T(8,128)}, f32[32,1024]{1,0:T(8,128)}, f32[1,1024]{1,0:T(1,128)}) custom-call(f32[72,1024]{1,0:T(8,128)S(1)} %shard_map.94.sums), custom_call_target="tpu_custom_call" | custom-call | tf_op jit(solution)/shard_map/pallas_call | solution.py:641

commit v4 on v3

--- a/solution.py
+++ b/solution.py
@@ -37,8 +37,7 @@
     x_ref, dn_ref, up_ref, gain_ref, head_ref, lab_ref, val_ref,
     odn, oup, ogain, stok, rtok, ssq, rsq, sgram, rgram, pgram, gall, sres, res,
     sdp, rnear, rfar, relay, psum, rcross, sgn, rsm, spr, rgn,
-    load, sib_s, sib_r, tok_s, tok_r, sq_s, sq_r, gr_s, gr_r, gq_s, gq_r, ga_s, ga_r, gf_s, gf_r, gc_s, gc_r,
-    re_s, re_r, fw_s, fw_r, dp_s, dp_r, far_s, far_r, rel_s, rel_r, cr_s, cr_r, sm_s, sm_r, su_s, su_r,
+    bulk, load, plane_s, sib_s, sib_r, tok_r, gr_r, gq_r, ga_r, gf_r, gc_r, re_r, fw_r, la_r, dp_s, dp_r, far_s, far_r, rel_s, rel_r, cr_s, cr_r, sm_s, sm_r, su_s, su_r,
 ):
     s, d, t = lax.axis_index("section"), lax.axis_index("dp"), lax.axis_index("tensor")
     first = s == 0
@@ -49,6 +48,8 @@
     rows = rank // nt
     part = rank // nd
     wire = stok.dtype
+    own_size, rows_size = (n * rank * wire.itemsize for n in (own, rows))
+    tok_size = (3 * (nt - 1) + 2 * nt) * own_size + (nt - 1) * 16 * half * wire.itemsize
 
     hl = nd // 2
     quarter = hl // 2
@@ -68,10 +69,10 @@
         return lax.rem(t + nt - k, nt)
 
     loads = [
-        pltpu.make_async_copy(a, b, load.at[i])
+        pltpu.make_async_copy(a, b, load.at[min(i, 5)])
         for i, (a, b) in enumerate((
-            (up_hbm, up_ref), (head_hbm, head_ref), (x_hbm, x_ref), (gain_hbm, gain_ref),
-            (dn_hbm, dn_ref), (lab_hbm, lab_ref), (val_hbm, val_ref),
+            (up_hbm, up_ref), (head_hbm, head_ref), (gain_hbm, gain_ref), (lab_hbm, lab_ref), (val_hbm, val_ref),
+            (x_hbm, x_ref), (dn_hbm, dn_ref),
         ))
     ]
     for c in loads:
@@ -93,6 +94,9 @@
         return pltpu.make_async_remote_copy(
             src_ref=src, dst_ref=dst, send_sem=ss, recv_sem=rs, device_id=(section, d, column), device_id_type=MESH
         )
+
+    def block(size):
+        return bulk.at[pl.ds(0, size // (4 * bulk.shape[1] * bulk.shape[2]))]
 
     def whole(ref, sem):
         return copy(ref, ref, sem, sem, 1 - s, t)
@@ -119,41 +123,41 @@
 
     def sib(i):
         a, b = ((up_ref, oup), (dn_ref, odn), (gain_ref, ogain))[i]
-        return copy(a, b, sib_s.at[i], sib_r.at[i], 1 - s, t)
+        return copy(a, b, sib_s if i == 2 else plane_s, sib_r.at[i], 1 - s, t)
 
     def ab_scatter(k, sender):
         return copy(
-            sgram.at[ahead(k), pl.ds(0, 2)], rgram.at[sender, k, pl.ds(0, 2)], gr_s, gr_r.at[sender], 1, ahead(k)
+            sgram.at[ahead(k), pl.ds(0, 2)], rgram.at[sender, k, pl.ds(0, 2)], plane_s, gr_r, 1, ahead(k)
         )
 
     def cd_scatter(k):
-        return copy(sgram.at[ahead(k), pl.ds(2, 2)], rgram.at[1, k, pl.ds(2, 2)], gq_s, gq_r, 1, ahead(k))
+        return copy(sgram.at[ahead(k), pl.ds(2, 2)], rgram.at[1, k, pl.ds(2, 2)], plane_s, gq_r, 1, ahead(k))
 
     def tok_cross(k):
         block = pl.ds(0, 2)
         return copy(
-            stok.at[1 - s, ahead(k), block], rtok.at[1, k, block], tok_s.at[1], tok_r.at[1], 1 - s, ahead(k)
+            stok.at[1 - s, ahead(k), block], rtok.at[1, k, block], plane_s, tok_r, 1 - s, ahead(k)
         )
 
     def tok_own(k):
-        return copy(stok.at[s, ahead(k)], rtok.at[0, k], tok_s.at[0], tok_r.at[0], s, ahead(k))
+        return copy(stok.at[s, ahead(k)], rtok.at[0, k], plane_s, tok_r, s, ahead(k))
 
     def sq_own(k):
-        return copy(ssq, rsq.at[k], sq_s, sq_r, s, ahead(k))
+        return copy(ssq, rsq.at[k], plane_s, tok_r, s, ahead(k))
 
     ab_all = gall.at[:, pl.ds(0, 4)]
     cd_all = gall.at[:, pl.ds(4, 2)]
 
     def ab_gather(k):
         block = pl.ds(0, 4)
-        return copy(pgram.at[block], gall.at[t, block], ga_s, ga_r, 1, ahead(k))
+        return copy(pgram.at[block], gall.at[t, block], plane_s, ga_r, 1, ahead(k))
 
     def ab_forward():
-        return copy(ab_all, ab_all, gf_s, gf_r, 0, t)
+        return copy(ab_all, ab_all, plane_s, gf_r, 0, t)
 
     def cd_gather(k, section):
         block = pl.ds(4, 2)
-        return copy(pgram.at[block], gall.at[t, block], gc_s.at[section], gc_r, section, ahead(k))
+        return copy(pgram.at[block], gall.at[t, block], plane_s, gc_r, section, ahead(k))
 
     sib(0).start()
     for k in range(1, nt):
@@ -163,8 +167,9 @@
     def _():
         ab_scatter(0, 0).start()
 
-    for c in loads[2:]:
+    for c in loads[2:5]:
         c.wait()
+    pltpu.make_async_copy(block(2 * tokens * feats + 2 * rank * feats), block(2 * tokens * feats + 2 * rank * feats), load.at[5]).wait()
     gain = gain_ref[...].astype(F32)
     xb = x_ref[...]
     xf = xb.astype(F32)
@@ -206,11 +211,10 @@
     def _():
         sib(1).start()
         sib(2).start()
-        arrived(rgram.at[1, pl.ds(1, nt - 1), pl.ds(0, 2)], gr_r.at[1])
+        arrived(block((2 * nt - 1) * 2 * rows_size), gr_r)
         mine1 = sgram[t, 0:2].astype(F32)
         for k in range(1, nt):
             mine1 = mine1 + rgram[1, k, 0:2].astype(F32)
-        arrived(rgram.at[0, :, pl.ds(0, 2)], gr_r.at[0])
         mine0 = rgram[0, 0, 0:2].astype(F32)
         for k in range(1, nt):
             mine0 = mine0 + rgram[0, k, 0:2].astype(F32)
@@ -245,11 +249,10 @@
     validity = mm_nt(pick, val_t)
     count = jnp.sum(val_ref[...].astype(F32))
 
-    arrived(rtok.at[0, pl.ds(1, nt - 1)], tok_r.at[0])
+    arrived(block(tok_size), tok_r)
     mine = stok[s, t].astype(F32)
     for k in range(1, nt):
         mine = mine + rtok[0, k].astype(F32)
-    arrived(rtok.at[1, :, pl.ds(0, 2)], tok_r.at[1])
     theirs = rtok[1, 0, 0:2].astype(F32)
     for k in range(1, nt):
         theirs = theirs + rtok[1, k, 0:2].astype(F32)
@@ -258,7 +261,6 @@
     v0 = jnp.where(first, mine[1], theirs[1])
     v1 = jnp.where(first, theirs[1], mine[1])
     xh = mine[2]
-    arrived(rsq.at[pl.ds(1, nt - 1)], sq_r)
     sq = ssq[...].astype(F32)
     for k in range(1, nt):
         sq = sq + rsq[k].astype(F32)
@@ -289,7 +291,7 @@
 
     a0, b0, a1, b1, c0, d1 = (gram(j) for j in range(6))
 
-    parts = ((0, 2), (2, 4))
+    parts = ((0, 2), (2, 3))
 
     def keep(j, v):
         v = v.astype(wire)
@@ -299,12 +301,15 @@
     def shared(m, k):
         at, size = parts[m]
         span = pl.ds(at, size)
-        return copy(sres.at[span], res.at[s, t, span], re_s.at[m], re_r.at[m, s], 1, ahead(k))
-
-    def onward(m, b):
+        return copy(sres.at[span], res.at[s, t, span], plane_s, re_r.at[m], 1, ahead(k))
+
+    def onward(m):
         at, size = parts[m]
-        block = res.at[b, :, pl.ds(at, size)]
-        return copy(block, block, fw_s.at[m], fw_r.at[m], 0, t)
+        blocks = res.at[:, :, pl.ds(at, size)]
+        return copy(blocks, blocks, plane_s, fw_r.at[m], 0, t)
+
+    def last(k):
+        return copy(sres.at[5], res.at[s, t, 5], plane_s, la_r, 0, ahead(k))
 
     def share(m):
         for k in range(1, nt):
@@ -353,11 +358,17 @@
         lane < q4, ch_h.astype(F32),
         jnp.where(lane < 2 * q4, ch_l.astype(F32), jnp.where(lane < 3 * q4, c1_h.astype(F32), c1_l.astype(F32))),
     ))
+    share(1)
     hg0 = mm_nt(wh, b0) - ch * yu0 + mm_nt(w1, d1) - c1 * s1u0
     act0 = hg0 * sig0 * (1.0 + pre0 * (1.0 - sig0))
     w0 = (inv0 * act0).astype(BF16)
     keep(5, w0)
-    share(1)
+    for k in range(1, nt):
+        last(k).start()
+
+    @pl.when(s != 0)
+    def _():
+        last(0).start()
 
     def got(j):
         return res[:, :, j].reshape(tokens, res.shape[-1])
@@ -405,14 +416,27 @@
             at, size = parts[m]
             span = pl.ds(at, size)
             if sec:
-                arrived(res.at[1, pl.ds(1, nt - 1), span], re_r.at[m, 1])
-                onward(m, 1).start()
-                arrived(res.at[0, :, span], re_r.at[m, 0])
-                onward(m, 0).start()
+                arrived(block((2 * nt - 1) * size * own_size), re_r.at[m])
+                onward(m).start()
             else:
                 arrived(res.at[:, :, span], fw_r.at[m])
 
+        def down(state, own_w):
+            piece(0, mm_tn(own_w, (state * gain).astype(BF16)))
+
+            @pl.when(outer)
+            def _():
+                relay_copy(0).start()
+
+            @pl.when(jnp.logical_not(outer))
+            def _():
+                for k in range(1, hl):
+                    near_copy(k, 0).start()
+
         if sec == 0:
+            arrived(block((2 * nt - 1) * own_size), la_r)
+            state, own_w = xf, got(5).astype(BF16)
+            down(state, own_w)
             for i in range(3):
                 sib(i).wait_recv()
         collect(0)
@@ -421,18 +445,9 @@
         y = s1 + mm(h1g, u1[...])
         collect(1)
         w1g = got(3).astype(BF16)
-        state, own_w = (s1, w1g) if sec else (xf, got(5).astype(BF16))
-        piece(0, mm_tn(own_w, (state * gain).astype(BF16)))
-
-        @pl.when(outer)
-        def _():
-            relay_copy(0).start()
-
-        @pl.when(jnp.logical_not(outer))
-        def _():
-            for k in range(1, hl):
-                near_copy(k, 0).start()
-
+        if sec:
+            state, own_w = s1, w1g
+            down(state, own_w)
         cg = got(4).astype(F32)
         chg = cg[:, 0:1] + cg[:, q4 : q4 + 1]
         g = mm_nt(got(2).astype(BF16), head_ref[...]) - chg * y
@@ -452,21 +467,21 @@
     def _():
         tail(1)
 
-    @pl.when(outer)
-    def _():
+    def end(sec):
         small_first().start()
-        queue = [relay_copy(0), relay_copy(1), relay_copy(2)]
+        queue = [relay_copy(g) for g in range(3)]
         queue += [up_copy(i) for i in range(quarter)]
         queue += [near_copy(k, j) for j in (1, 0) for k in range(1, hl)]
+        window = 6 if sec else 3
         for i in range(1, len(queue)):
-            if i >= 2:
-                queue[i - 2].wait_send()
+            if i >= window:
+                queue[i - window].wait_send()
             queue[i].start()
-        for c in queue[max(0, len(queue) - 2):]:
+        for c in queue[-window:]:
             c.wait_send()
-
-    @pl.when(jnp.logical_not(outer))
-    def _():
+        small_first().wait_send()
+
+    def middle(sec):
         for i in range(quarter):
             up_copy(i).start()
         for k in range(1, hl):
@@ -482,6 +497,16 @@
                 psum[g, i] = (sdp[at, 1 if g == 1 else 0].astype(F32) + relay[g, i].astype(F32)).astype(BF16)
                 cross_copy(g, i).start()
 
+    for sec in (0, 1):
+
+        @pl.when(jnp.logical_and(outer, s == sec))
+        def _():
+            end(sec)
+
+        @pl.when(jnp.logical_and(jnp.logical_not(outer), s == sec))
+        def _():
+            middle(sec)
+
     rgn_own = d // 2
 
     @pl.when(outer)
@@ -521,10 +546,6 @@
 
     total(0, True)
 
-    @pl.when(outer)
-    def _():
-        small_first().wait_send()
-
     @pl.when(jnp.logical_not(outer))
     def _():
         for i in range(quarter):
@@ -535,30 +556,18 @@
             near_copy(k, 0).wait_send()
         sent(rgn.at[pl.ds(1, nd - 1)], sm_s)
 
-    sib(0).wait_send()
-    sent(rtok.at[0, pl.ds(1, nt - 1)], tok_s.at[0])
-    sent(rtok.at[1, :, pl.ds(0, 2)], tok_s.at[1])
-    sent(rsq.at[pl.ds(1, nt - 1)], sq_s)
+    common = 2 * rank * feats + tok_size
 
     @pl.when(first)
     def _():
-        sent(rgram.at[0, :, pl.ds(0, 2)], gr_s)
-        for m, (at, size) in enumerate(parts):
-            sent(res.at[0, :, pl.ds(at, size)], re_s.at[m])
+        sent(block(common + 2 * nt * rows_size + (6 * nt - 1) * own_size), plane_s)
 
     @pl.when(s != 0)
     def _():
-        sib(1).wait_send()
         sib(2).wait_send()
-        sent(rgram.at[1, pl.ds(1, nt - 1), pl.ds(0, 2)], gr_s)
-        sent(rgram.at[1, pl.ds(1, nt - 1), pl.ds(2, 2)], gq_s)
-        sent(gall.at[pl.ds(1, nt - 1), pl.ds(0, 4)], ga_s)
-        ab_forward().wait_send()
-        sent(cd_all, gc_s.at[0])
-        sent(gall.at[pl.ds(1, nt - 1), pl.ds(4, 2)], gc_s.at[1])
-        for m, (at, size) in enumerate(parts):
-            sent(res.at[1, pl.ds(1, nt - 1), pl.ds(at, size)], re_s.at[m])
-            sent(res.at[:, :, pl.ds(at, size)], fw_s.at[m])
+        grams = 10 * (nt - 1) + 6 * nt
+        results = 5 * (nt - 1) + nt + 10 * nt
+        sent(block(common + 2 * rank * feats + grams * rows_size + results * own_size), plane_s)
 
 
 def scale_kernel(part, sums, down_out, up_out, gain_out):
@@ -579,6 +588,8 @@
         rank = down.shape[2]
         own, rows, part = tokens // ns // nt, rank // nt, rank // nd
         wire = BF16 if own % 16 == 0 and rows % 16 == 0 else F32
+        bulk = (4 * rank + 2 * tokens) * feats + (27 * nt + 16 * nt * rows) * rank * 4 + 64 * nt * own * rank
+        bulk = bulk // 2048 + nt * 16 * tokens // 1024
         vmem = pl.BlockSpec(memory_space=pltpu.VMEM)
         dma = pltpu.SemaphoreType.DMA
         anyspace = pl.BlockSpec(memory_space=pl.ANY)
@@ -618,17 +629,11 @@
                 pltpu.VMEM((2, feats), F32),
                 pltpu.VMEM((2, feats), F32),
                 pltpu.VMEM((nd, 2, feats), F32),
-                dma((7,)),
-                dma((3,)), dma((3,)),
-                dma((2,)), dma((2,)),
-                dma, dma,
-                dma, dma((2,)),
-                dma, dma,
-                dma, dma,
-                dma, dma,
-                dma((2,)), dma,
-                dma((2,)), dma((2, 2)),
-                dma((2,)), dma((2,)),
+                pltpu.VMEM((bulk, 8, 128), F32),
+                dma((6,)),
+                dma, dma, dma((3,)),
+                dma, dma, dma, dma, dma, dma,
+                dma((2,)), dma((2,)), dma,
                 dma((2, nd // 2 - 1)), dma((2,)),
                 dma((nd // 4,)), dma,
                 dma((3,)), dma((3,)),

time: 30.1 us -> 29.9 us (level)
  no operation moved by 1% of the time
where the time goes in v4:
time: 29.9 us; the launch traced here: 29.8 us
  Pallas kernels  29.1 us (97%)
  between operations  0.64 us (2%)
    pallas_call x1, Pallas kernels, local(): pl.pallas_call(functools.partial(kernel, nt, nd, feats * nt), out_shape=p...  28.4 us
    pallas_call x1, Pallas kernels, local(): pl.pallas_call(functools.partial(scale_kernel, part), out_shape=(jax.Shap...  0.72 us

profile of v4, /device:TPU:0, one launch (start us, length us, event | category | flops | bytes accessed | tf_op | source)
XLA Modules:
  0.0 29.8 jit_solution(13969416824023234416)
XLA Ops:
  0.6 28.4 %shard_map.94.sums = f32[72,1024]{1,0:T(8,128)S(1)} custom-call(bf16[256,1024]{1,0:T(8,128)(2,1)} %bitcast.7, bf16[1024,128]{1,0:T(8,128)(2,1)} %bitcast.8, bf16[128,1024]{1,0:T(8,128)(2,1)} %bitcast.9, bf16[1,1024]{1,0:T(2,128)(2,1)} %gain_hbm.1, bf16[1024,128]{1,0:T(8,128)(2,1)} %head_hbm.1, s32[2,128]{1,0:T(2,128)} %lab_hbm.1, s32[2,128]{1,0:T(2,128)} %val_hbm.1), custom_call_target="tpu_custom_call" | custom-call | tf_op jit(solution)/shard_map/pallas_call | solution.py:596
  29.0 0.7 %shard_map.95 = (f32[32,1024]{1,0:T(8,128)}, f32[32,1024]{1,0:T(8,128)}, f32[1,1024]{1,0:T(1,128)}) custom-call(f32[72,1024]{1,0:T(8,128)S(1)} %shard_map.94.sums), custom_call_target="tpu_custom_call" | custom-call | tf_op jit(solution)/shard_map/pallas_call | solution.py:646

commit v5 on v4

--- a/solution.py
+++ b/solution.py
@@ -37,7 +37,7 @@
     x_ref, dn_ref, up_ref, gain_ref, head_ref, lab_ref, val_ref,
     odn, oup, ogain, stok, rtok, ssq, rsq, sgram, rgram, pgram, gall, sres, res,
     sdp, rnear, rfar, relay, psum, rcross, sgn, rsm, spr, rgn,
-    bulk, load, plane_s, sib_s, sib_r, tok_r, gr_r, gq_r, ga_r, gf_r, gc_r, re_r, fw_r, la_r, dp_s, dp_r, far_s, far_r, rel_s, rel_r, cr_s, cr_r, sm_s, sm_r, su_s, su_r,
+    bulk, load, plane_s, sib_s, sib_r, tok_r, gr_r, gq_r, ga_r, gf_r, gc_r, re_r, fw_r, la_r, dp_s, dp_r, far_r, rel_r, cr_r, sm_s, sm_r, su_s, su_r,
 ):
     s, d, t = lax.axis_index("section"), lax.axis_index("dp"), lax.axis_index("tensor")
     first = s == 0
@@ -388,19 +388,19 @@
 
     def near_copy(k, j):
         to = side * hl + lax.rem(local_d + k, hl)
-        return remote(sdp.at[to, j], rnear.at[j, k], dp_s.at[j, k - 1], dp_r.at[j], to)
+        return remote(sdp.at[to, j], rnear.at[j, k], dp_s, dp_r.at[j], to)
 
     def up_copy(i):
-        return remote(sdp.at[near_far + i, 1], rfar.at[local_d], far_s.at[i], far_r, near_far + i)
+        return remote(sdp.at[near_far + i, 1], rfar.at[local_d], dp_s, far_r, near_far + i)
 
     def relay_copy(g):
         block = pl.ds(near_far if g == 2 else deep_far, quarter)
-        return remote(sdp.at[block, 1 if g == 1 else 0], relay.at[g], rel_s.at[g], rel_r.at[g], partner)
+        return remote(sdp.at[block, 1 if g == 1 else 0], relay.at[g], dp_s, rel_r.at[g], partner)
 
     def cross_copy(g, i):
         m = local_d // 2
         to = (near_far if g == 2 else deep_far) + i
-        return remote(psum.at[g, i], rcross.at[1 if g == 1 else 0, m], cr_s, cr_r.at[1 if g == 1 else 0], to)
+        return remote(psum.at[g, i], rcross.at[1 if g == 1 else 0, m], dp_s, cr_r.at[1 if g == 1 else 0], to)
 
     def small_copy(k):
         to = lax.rem(d + k, nd)
@@ -456,8 +456,8 @@
             g = g + ogain[...].astype(F32) * mm_nt(w1g, odn[...]) - c1g * s1
         piece(1, mm_tn(h1g if sec else h0g, g.astype(BF16)))
         gain_row = jnp.sum(mm_nt(own_w, dn_ref[...]) * state, axis=0, keepdims=True)
-        sgn[0:1, :] = gain_row
-        sgn[1:2, :] = jnp.full((1, feats), count, F32)
+        sgn[:, 0:feats] = gain_row
+        sgn[:, feats:] = jnp.full((1, 128), count, F32)
 
     @pl.when(first)
     def _():
@@ -469,16 +469,11 @@
 
     def end(sec):
         small_first().start()
-        queue = [relay_copy(g) for g in range(3)]
+        queue = [relay_copy(g) for g in (1, 2)]
         queue += [up_copy(i) for i in range(quarter)]
         queue += [near_copy(k, j) for j in (1, 0) for k in range(1, hl)]
-        window = 6 if sec else 3
-        for i in range(1, len(queue)):
-            if i >= window:
-                queue[i - window].wait_send()
-            queue[i].start()
-        for c in queue[-window:]:
-            c.wait_send()
+        for c in queue:
+            c.start()
         small_first().wait_send()
 
     def middle(sec):
@@ -519,7 +514,8 @@
     for j in range(1, nd // 2):
         p = lax.rem(rgn_own + j, nd // 2)
         small = small + rgn[p]
-    out[2 * part : 2 * part + 2, :] = small
+    out[2 * part : 2 * part + 1, :] = small[:, 0:feats]
+    out[2 * part + 1 : 2 * part + 2, :] = jnp.broadcast_to(small[:, feats : feats + 1], (1, feats))
 
     def total(j, from_pairs):
         arrived(rnear.at[j, pl.ds(1, hl - 1)], dp_r.at[j])
@@ -548,15 +544,10 @@
 
     @pl.when(jnp.logical_not(outer))
     def _():
-        for i in range(quarter):
-            up_copy(i).wait_send()
-        sent(psum, cr_s)
-        for k in range(1, hl):
-            near_copy(k, 1).wait_send()
-            near_copy(k, 0).wait_send()
         sent(rgn.at[pl.ds(1, nd - 1)], sm_s)
 
     common = 2 * rank * feats + tok_size
+    sent(block((4 * quarter + 2 * (hl - 1)) * 2 * part * feats), dp_s)
 
     @pl.when(first)
     def _():
@@ -625,19 +616,16 @@
                 pltpu.VMEM((3, nd // 4, part, feats), BF16),
                 pltpu.VMEM((3, nd // 4, part, feats), BF16),
                 pltpu.VMEM((2, nd // 4, part, feats), BF16),
-                pltpu.VMEM((2, feats), F32),
-                pltpu.VMEM((2, feats), F32),
-                pltpu.VMEM((2, feats), F32),
-                pltpu.VMEM((nd, 2, feats), F32),
+                pltpu.VMEM((1, feats + 128), F32),
+                pltpu.VMEM((1, feats + 128), F32),
+                pltpu.VMEM((1, feats + 128), F32),
+                pltpu.VMEM((nd, 1, feats + 128), F32),
                 pltpu.VMEM((bulk, 8, 128), F32),
                 dma((6,)),
                 dma, dma, dma((3,)),
                 dma, dma, dma, dma, dma, dma,
                 dma((2,)), dma((2,)), dma,
-                dma((2, nd // 2 - 1)), dma((2,)),
-                dma((nd // 4,)), dma,
-                dma((3,)), dma((3,)),
-                dma, dma((2,)),
+                dma, dma((2,)), dma, dma((3,)), dma((2,)),
                 dma, dma((2,)),
                 dma, dma,
             ],

time: 29.9 us -> 29.7 us (level)
  no operation moved by 1% of the time
where the time goes in v5:
time: 29.7 us; the launch traced here: 29.5 us
  Pallas kernels  28.9 us (97%)
  between operations  0.64 us (2%)
    pallas_call x1, Pallas kernels, local(): pl.pallas_call(functools.partial(kernel, nt, nd, feats * nt), out_shape=p...  28.2 us
    pallas_call x1, Pallas kernels, local(): pl.pallas_call(functools.partial(scale_kernel, part), out_shape=(jax.Shap...  0.72 us

profile of v5, /device:TPU:0, one launch (start us, length us, event | category | flops | bytes accessed | tf_op | source)
XLA Modules:
  0.0 29.5 jit_solution(4944310181064707726)
XLA Ops:
  0.6 28.2 %shard_map.94.sums = f32[72,1024]{1,0:T(8,128)S(1)} custom-call(bf16[256,1024]{1,0:T(8,128)(2,1)} %bitcast.7, bf16[1024,128]{1,0:T(8,128)(2,1)} %bitcast.8, bf16[128,1024]{1,0:T(8,128)(2,1)} %bitcast.9, bf16[1,1024]{1,0:T(2,128)(2,1)} %gain_hbm.1, bf16[1024,128]{1,0:T(8,128)(2,1)} %head_hbm.1, s32[2,128]{1,0:T(2,128)} %lab_hbm.1, s32[2,128]{1,0:T(2,128)} %val_hbm.1), custom_call_target="tpu_custom_call" | custom-call | tf_op jit(solution)/shard_map/pallas_call | solution.py:587
  28.8 0.7 %shard_map.95 = (f32[32,1024]{1,0:T(8,128)}, f32[32,1024]{1,0:T(8,128)}, f32[1,1024]{1,0:T(1,128)}) custom-call(f32[72,1024]{1,0:T(8,128)S(1)} %shard_map.94.sums), custom_call_target="tpu_custom_call" | custom-call | tf_op jit(solution)/shard_map/pallas_call | solution.py:634

commit v6 on v5

--- a/solution.py
+++ b/solution.py
@@ -180,7 +180,7 @@
             at = b * half + i * own
             stok[b, i, 0] = proj[at : at + own]
             stok[b, i, 1] = xup[at : at + own]
-    for k in range(nt):
+    for k in list(range(1, nt)) + [0]:
         tok_cross(k).start()
 
     xm = x_ref[pl.ds(pl.multiple_of(s * half, half), half), :]
@@ -421,8 +421,8 @@
             else:
                 arrived(res.at[:, :, span], fw_r.at[m])
 
-        def down(state, own_w):
-            piece(0, mm_tn(own_w, (state * gain).astype(BF16)))
+        def down(scaled, own_w):
+            piece(0, mm_tn(own_w, scaled))
 
             @pl.when(outer)
             def _():
@@ -436,18 +436,19 @@
         if sec == 0:
             arrived(block((2 * nt - 1) * own_size), la_r)
             state, own_w = xf, got(5).astype(BF16)
-            down(state, own_w)
+            down((state * gain).astype(BF16), own_w)
             for i in range(3):
                 sib(i).wait_recv()
         collect(0)
         h0g, h1g = got(0).astype(BF16), got(1).astype(BF16)
         s1 = xf + mm(h0g, u0[...])
         y = s1 + mm(h1g, u1[...])
+        scaled = (s1 * gain).astype(BF16) if sec else None
         collect(1)
         w1g = got(3).astype(BF16)
         if sec:
             state, own_w = s1, w1g
-            down(state, own_w)
+            down(scaled, own_w)
         cg = got(4).astype(F32)
         chg = cg[:, 0:1] + cg[:, q4 : q4 + 1]
         g = mm_nt(got(2).astype(BF16), head_ref[...]) - chg * y
@@ -470,7 +471,7 @@
     def end(sec):
         small_first().start()
         queue = [relay_copy(g) for g in (1, 2)]
-        queue += [up_copy(i) for i in range(quarter)]
+        queue = queue[:1] + [up_copy(i) for i in range(quarter)] + queue[1:]
         queue += [near_copy(k, j) for j in (1, 0) for k in range(1, hl)]
         for c in queue:
             c.start()

time: 29.7 us -> 29.6 us (level)
  no operation moved by 1% of the time
where the time goes in v6:
time: 29.6 us; the launch traced here: 29.5 us
  Pallas kernels  28.8 us (97%)
  between operations  0.64 us (2%)
    pallas_call x1, Pallas kernels, local(): pl.pallas_call(functools.partial(kernel, nt, nd, feats * nt), out_shape=p...  28.1 us
    pallas_call x1, Pallas kernels, local(): pl.pallas_call(functools.partial(scale_kernel, part), out_shape=(jax.Shap...  0.72 us

profile of v6, /device:TPU:0, one launch (start us, length us, event | category | flops | bytes accessed | tf_op | source)
XLA Modules:
  0.0 29.5 jit_solution(482586188514937864)
XLA Ops:
  0.6 28.1 %shard_map.94.sums = f32[72,1024]{1,0:T(8,128)S(1)} custom-call(bf16[256,1024]{1,0:T(8,128)(2,1)} %bitcast.7, bf16[1024,128]{1,0:T(8,128)(2,1)} %bitcast.8, bf16[128,1024]{1,0:T(8,128)(2,1)} %bitcast.9, bf16[1,1024]{1,0:T(2,128)(2,1)} %gain_hbm.1, bf16[1024,128]{1,0:T(8,128)(2,1)} %head_hbm.1, s32[2,128]{1,0:T(2,128)} %lab_hbm.1, s32[2,128]{1,0:T(2,128)} %val_hbm.1), custom_call_target="tpu_custom_call" | custom-call | tf_op jit(solution)/shard_map/pallas_call | solution.py:588
  28.7 0.7 %shard_map.95 = (f32[32,1024]{1,0:T(8,128)}, f32[32,1024]{1,0:T(8,128)}, f32[1,1024]{1,0:T(1,128)}) custom-call(f32[72,1024]{1,0:T(8,128)S(1)} %shard_map.94.sums), custom_call_target="tpu_custom_call" | custom-call | tf_op jit(solution)/shard_map/pallas_call | solution.py:635

commit v7 on v6

--- a/solution.py
+++ b/solution.py
@@ -37,7 +37,7 @@
     x_ref, dn_ref, up_ref, gain_ref, head_ref, lab_ref, val_ref,
     odn, oup, ogain, stok, rtok, ssq, rsq, sgram, rgram, pgram, gall, sres, res,
     sdp, rnear, rfar, relay, psum, rcross, sgn, rsm, spr, rgn,
-    bulk, load, plane_s, sib_s, sib_r, tok_r, gr_r, gq_r, ga_r, gf_r, gc_r, re_r, fw_r, la_r, dp_s, dp_r, far_r, rel_r, cr_r, sm_s, sm_r, su_s, su_r,
+    bulk, load, plane_s, sib_s, sib_r, tok_r, gr_r, gq_r, ga_r, gc_r, re_r, fw_r, la_r, dp_s, dp_r, far_r, rel_r, cr_r, sm_s, sm_r, su_r,
 ):
     s, d, t = lax.axis_index("section"), lax.axis_index("dp"), lax.axis_index("tensor")
     first = s == 0
@@ -75,8 +75,7 @@
             (x_hbm, x_ref), (dn_hbm, dn_ref),
         ))
     ]
-    for c in loads:
-        c.start()
+    loads[0].start()
 
     barrier = pltpu.get_barrier_semaphore()
     for k in range(1, nd):
@@ -89,6 +88,9 @@
     group = [(k, o) for k in range(nt) for o in (0, 1) if (k, o) != (0, 0)]
     for k, o in group:
         pl.semaphore_signal(barrier, inc=1, device_id=(1 - s if o else s, d, ahead(k)), device_id_type=MESH)
+
+    for c in loads[1:]:
+        c.start()
 
     def copy(src, dst, ss, rs, section, column):
         return pltpu.make_async_remote_copy(
@@ -123,7 +125,7 @@
 
     def sib(i):
         a, b = ((up_ref, oup), (dn_ref, odn), (gain_ref, ogain))[i]
-        return copy(a, b, sib_s if i == 2 else plane_s, sib_r.at[i], 1 - s, t)
+        return copy(a, b, sib_s if i == 2 else plane_s, sib_r.at[i // 2], 1 - s, t)
 
     def ab_scatter(k, sender):
         return copy(
@@ -153,7 +155,7 @@
         return copy(pgram.at[block], gall.at[t, block], plane_s, ga_r, 1, ahead(k))
 
     def ab_forward():
-        return copy(ab_all, ab_all, plane_s, gf_r, 0, t)
+        return copy(ab_all, ab_all, plane_s, gc_r, 0, t)
 
     def cd_gather(k, section):
         block = pl.ds(4, 2)
@@ -283,8 +285,7 @@
 
     @pl.when(first)
     def _():
-        ab_forward().wait_recv()
-        arrived(cd_all, gc_r)
+        arrived(block(6 * nt * rows_size), gc_r)
 
     def gram(j):
         return gall[:, j].reshape(rank, rank).astype(BF16)
@@ -407,7 +408,7 @@
         return remote(spr, rgn.at[d // 2], sm_s, sm_r.at[(to // 2 != d // 2).astype(jnp.int32)], to)
 
     def small_first():
-        return remote(sgn, rsm, su_s, su_r, partner)
+        return remote(sgn, rsm, sm_s, su_r, partner)
 
     def tail(sec):
         u0, u1 = (oup, up_ref) if sec else (up_ref, oup)
@@ -437,8 +438,8 @@
             arrived(block((2 * nt - 1) * own_size), la_r)
             state, own_w = xf, got(5).astype(BF16)
             down((state * gain).astype(BF16), own_w)
-            for i in range(3):
-                sib(i).wait_recv()
+            arrived(block(4 * rank * feats), sib_r.at[0])
+            sib(2).wait_recv()
         collect(0)
         h0g, h1g = got(0).astype(BF16), got(1).astype(BF16)
         s1 = xf + mm(h0g, u0[...])
@@ -623,12 +624,11 @@
                 pltpu.VMEM((nd, 1, feats + 128), F32),
                 pltpu.VMEM((bulk, 8, 128), F32),
                 dma((6,)),
-                dma, dma, dma((3,)),
-                dma, dma, dma, dma, dma, dma,
+                dma, dma, dma((2,)),
+                dma, dma, dma, dma, dma,
                 dma((2,)), dma((2,)), dma,
                 dma, dma((2,)), dma, dma((3,)), dma((2,)),
-                dma, dma((2,)),
-                dma, dma,
+                dma, dma((2,)), dma,
             ],
             compiler_params=pltpu.CompilerParams(collective_id=0, has_side_effects=True),
         )(inputs.reshape(tokens, feats), down[0], up[0], gains, head, labels, valid)

time: 29.6 us -> 29.6 us (level)
  no operation moved by 1% of the time
where the time goes in v7:
time: 29.6 us; the launch traced here: 29.4 us
  Pallas kernels  28.8 us (97%)
  between operations  0.64 us (2%)
    pallas_call x1, Pallas kernels, local(): pl.pallas_call(functools.partial(kernel, nt, nd, feats * nt), out_shape=p...  28.1 us
    pallas_call x1, Pallas kernels, local(): pl.pallas_call(functools.partial(scale_kernel, part), out_shape=(jax.Shap...  0.72 us

profile of v7, /device:TPU:0, one launch (start us, length us, event | category | flops | bytes accessed | tf_op | source)
XLA Modules:
  0.0 29.4 jit_solution(11672805893436154524)
XLA Ops:
  0.6 28.1 %shard_map.94.sums = f32[72,1024]{1,0:T(8,128)S(1)} custom-call(bf16[256,1024]{1,0:T(8,128)(2,1)} %bitcast.7, bf16[1024,128]{1,0:T(8,128)(2,1)} %bitcast.8, bf16[128,1024]{1,0:T(8,128)(2,1)} %bitcast.9, bf16[1,1024]{1,0:T(2,128)(2,1)} %gain_hbm.1, bf16[1024,128]{1,0:T(8,128)(2,1)} %head_hbm.1, s32[2,128]{1,0:T(2,128)} %lab_hbm.1, s32[2,128]{1,0:T(2,128)} %val_hbm.1), custom_call_target="tpu_custom_call" | custom-call | tf_op jit(solution)/shard_map/pallas_call | solution.py:589
  28.7 0.7 %shard_map.95 = (f32[32,1024]{1,0:T(8,128)}, f32[32,1024]{1,0:T(8,128)}, f32[1,1024]{1,0:T(1,128)}) custom-call(f32[72,1024]{1,0:T(8,128)S(1)} %shard_map.94.sums), custom_call_target="tpu_custom_call" | custom-call | tf_op jit(solution)/shard_map/pallas_call | solution.py:635
